TPU v7x, 32 devices: a whole 2x2x4 slice. The times are simulated.
32 devices in a mesh: seq: 16 (over z, y, x), mp: 2 (over core).
Axes of the slice: x: 2, y: 2, z: 4, core: 2. Of those that a mesh axis runs over, the one named last changes fastest.
Arguments:
- states: bfloat16 [4096, 768], P('seq'), may hold values from -24 to 24
- qkv_weight: bfloat16 [3, 768, 768], P(None, None, 'mp'), may hold values from -0.21875 to 0.21875
- out_weight: bfloat16 [768, 768], P('mp'), may hold values from -0.21875 to 0.21875
- up_weight: bfloat16 [768, 3072], P(None, 'mp'), may hold values from -0.21875 to 0.21875
- down_weight: bfloat16 [3072, 768], P('mp'), may hold values from -0.109375 to 0.109375
- attn_gain: float32 [768], replicated, may hold values from 0.5 to 1.5
- mlp_gain: float32 [768], replicated, may hold values from 0.5 to 1.5
- global_ids: int32 [2], replicated, may hold values from 0 to 63, as said below
- random_owner: int32 [2, 64, 6, 3], P('mp', 'seq'), may hold values from 0 to 15, all different within a row; in each aligned block of 24 rows (0 to 23, 24 to 47, ..., all dimensions but the last counted through in order) at most 5 rows name the same one
- random_local: int32 [2, 64, 6, 3], P('mp', 'seq'), may hold values from 0 to 3
Outputs:
- layer_out: bfloat16 [4096, 768], P('seq')
Inputs may be any that keep to these rules, and one draw needn't show every extreme that they name: `global_ids`: 2 different block numbers; the second is 63. The random key block is random_owner * 4 + random_local. For one query block and head the 3 owners differ. Within the rows of one device (aligned blocks of 4 * K rows over the first three dimensions, K the third dimension) no owner is named more than 5 times, a bound that some block reaches.
All inputs are finite; a program needn't handle non-finite values.
Results may differ from a plain program's by a relative error of at most 0.008.
The roundings to bfloat16 on the way count: a program that leaves them out, or rounds other values in their place, can miss the bound.
Values may be sent and summed in bfloat16 or wider, within the bound.
A program may use at most 192 MiB of HBM per device.

v0:
```python
import functools

import jax
import jax.numpy as jnp
from jax import lax
from jax.experimental import pallas as pl
from jax.experimental.pallas import tpu as pltpu
from jax.sharding import PartitionSpec as P

HD = 64
BS = 64
R = 3
LANES = 128
MESH = pl.DeviceIdType.MESH

EPSILON = 1e-05
NEGATIVE = -1e30


def layer_norm(inputs, scales):
    center = jnp.mean(inputs, axis=-1, keepdims=True)
    shifted = inputs - center
    spread = jnp.mean(shifted * shifted, axis=-1, keepdims=True)
    return shifted * lax.rsqrt(spread + EPSILON) * scales


def dot_t(a, b):
    return lax.dot_general(a, b, (((1,), (1,)), ((), ())), preferred_element_type=jnp.float32)


def dot(a, b):
    return jnp.dot(a, b, preferred_element_type=jnp.float32)


def swap_halves(x):
    return pltpu.roll(x, HD, 1)


def attend_kernel(
    n,
    cap,
    heads,
    blocks,
    g_count,
    states_hbm,
    weight_hbm,
    wanted,
    slot,
    gids,
    att,
    states,
    weight,
    tab,
    tab_s,
    cand,
    cand_in,
    pick,
    gath,
    gstates,
    kvb,
    qpad,
    stage,
    rr,
    halo_l,
    halo_r,
    win,
    gq,
    gkv,
    part,
    part_in,
    gmine,
    gout,
    scores,
    s_tab,
    r_tab,
    s_cand,
    r_cand,
    s_gath,
    r_gath,
    s_rand,
    r_rand,
    s_halo,
    r_halo,
    s_part,
    r_part,
    s_gout,
    r_gout,
    s_mp,
    r_mp,
    l_sem,
    w_sem,
):
    me = lax.axis_index("seq")
    mine = lax.axis_index("mp")
    pairs = heads // 2
    width = states.shape[1]
    cols = width // LANES
    quarters = BS // 16
    half = gath.shape[0]
    gper = gath.shape[1] // (cols * quarters)
    units = gper * cols * quarters
    per = cand_in.shape[1]
    cand_parts = units // per
    rows_per = part_in.shape[2]
    part_parts = part.shape[0]
    left = lax.rem(me + n - 1, n)
    right = lax.rem(me + 1, n)

    def peer(k):
        return lax.rem(me + k, n)

    def each_peer(body):
        def step(k, carry):
            body(peer(k))
            return carry

        lax.fori_loop(1, n, step, 0)

    def guarded(limit, who, body):
        if limit < n:
            pl.when(who < limit)(body)
        else:
            body()

    def remote(src, dst, ssem, rsem, d):
        return pltpu.make_async_remote_copy(
            src_ref=src,
            dst_ref=dst,
            send_sem=ssem,
            recv_sem=rsem,
            device_id={"seq": d},
            device_id_type=MESH,
        )

    def tab_copy(d, owner):
        return remote(wanted.at[d], tab.at[owner], s_tab.at[d], r_tab.at[owner], d)

    def cand_copy(d, owner, at):
        return remote(
            cand.at[pl.ds(at * per, per)], cand_in.at[owner], s_cand.at[d], r_cand.at[owner], d
        )

    def gath_copy(d, owner):
        return remote(
            pick, gath.at[mine, pl.ds(owner * per, per)], s_gath.at[d], r_gath.at[owner], d
        )

    def rand_copy(d, owner):
        return remote(
            stage.at[pl.ds(d * cap, cap)],
            rr.at[pl.ds(owner * cap, cap)],
            s_rand.at[d],
            r_rand.at[owner],
            d,
        )

    def part_copy(d, owner, at):
        return remote(part.at[at], part_in.at[owner], s_part.at[d], r_part.at[owner], d)

    def gout_copy(d, owner):
        return remote(gmine, gout.at[owner], s_gout.at[d], r_gout.at[owner], d)

    def mp_copy(k, owner):
        other = lax.rem(mine + k, half)
        return pltpu.make_async_remote_copy(
            src_ref=gath.at[mine],
            dst_ref=gath.at[owner],
            send_sem=s_mp.at[k],
            recv_sem=r_mp.at[owner],
            device_id={"mp": other},
            device_id_type=MESH,
        )

    to_right = remote(
        kvb.at[pl.ds((blocks - 1) * heads, heads)], halo_l, s_halo.at[0], r_halo.at[0], right
    )
    to_left = remote(kvb.at[pl.ds(0, heads)], halo_r, s_halo.at[1], r_halo.at[1], left)

    loads = [pltpu.make_async_copy(states_hbm, states, w_sem.at[3])] + [
        pltpu.make_async_copy(weight_hbm.at[i], weight.at[i], w_sem.at[i]) for i in (1, 2, 0)
    ]
    for load in loads:
        load.start()

    barrier = pltpu.get_barrier_semaphore()
    each_peer(
        lambda d: pl.semaphore_signal(barrier, inc=1, device_id={"seq": d}, device_id_type=MESH)
    )
    for k in range(1, half):
        pl.semaphore_signal(
            barrier, inc=1, device_id={"mp": lax.rem(mine + k, half)}, device_id_type=MESH
        )

    loads[0].wait()
    for i in range(gper):
        local = lax.rem(gids[mine * gper + i], blocks)
        for j in range(cols):
            cut = slice(j * LANES, (j + 1) * LANES)
            piece = states[0:BS, cut]
            for b in range(1, blocks):
                piece = jnp.where(local == b, states[b * BS : (b + 1) * BS, cut], piece)
            for q in range(quarters):
                cand[(i * cols + j) * quarters + q] = piece[q * 16 : (q + 1) * 16]
    tab[me] = wanted[me]

    def own_cand():
        cand_in[me] = cand[pl.ds(me * per, per)]

    guarded(cand_parts, me, own_cand)
    loads[1].wait()
    loads[2].wait()

    lane = lax.broadcasted_iota(jnp.int32, (BS, LANES), 1)
    low = lane < HD
    x = states[...]
    for j in range(pairs):
        cut = slice(j * LANES, (j + 1) * LANES)
        k = dot(x, weight[1, :, cut])
        v = dot(x, weight[2, :, cut])
        for b in range(blocks):
            kb, vb = k[b * BS : (b + 1) * BS], v[b * BS : (b + 1) * BS]
            kvb[b * heads + 2 * j] = jnp.where(low, kb, swap_halves(vb)).astype(jnp.bfloat16)
            kvb[b * heads + 2 * j + 1] = jnp.where(low, swap_halves(kb), vb).astype(jnp.bfloat16)

    pl.semaphore_wait(barrier, n - 1 + half - 1)
    each_peer(lambda d: tab_copy(d, me).start())
    each_peer(lambda d: guarded(cand_parts, d, lambda: cand_copy(d, me, d).start()))
    to_right.start()
    to_left.start()

    loads[3].wait()
    scaling = HD ** (-0.5)
    for j in range(pairs):
        cut = slice(j * LANES, (j + 1) * LANES)
        q = dot(x, weight[0, :, cut]).astype(jnp.bfloat16).astype(jnp.float32) * scaling
        for b in range(blocks):
            qb = q[b * BS : (b + 1) * BS]
            qpad[b * heads + 2 * j] = jnp.where(low, qb, 0.0).astype(jnp.bfloat16)
            qpad[b * heads + 2 * j + 1] = jnp.where(low, swap_halves(qb), 0.0).astype(jnp.bfloat16)

    def relay():
        each_peer(lambda d: cand_copy(d, d, me).wait_recv())
        for u in range(per):
            g = (me * per + u) // (cols * quarters)
            wanted_id = gids[mine * gper + g]

            def choose(d, so_far):
                here = (wanted_id >= d * blocks) & (wanted_id < (d + 1) * blocks)
                return jnp.where(here, cand_in[d, u], so_far)

            pick[u] = lax.fori_loop(1, n, choose, cand_in[0, u])
        gath[mine, pl.ds(me * per, per)] = pick[...]
        each_peer(lambda d: gath_copy(d, me).start())

    guarded(cand_parts, me, relay)

    each_peer(lambda d: tab_copy(d, d).wait_recv())
    table = pltpu.make_async_copy(tab, tab_s, l_sem)
    table.start()
    table.wait()

    def serve(d):
        for c in range(cap):
            stage[d * cap + c] = kvb[tab_s[d, 0, c]]
        rand_copy(d, me).start()

    def serve_some(start, stop):
        def step(k, carry):
            serve(peer(k))
            return carry

        lax.fori_loop(start, stop, step, 0)

    for c in range(cap):
        rr[me * cap + c] = kvb[tab_s[me, 0, c]]

    each_peer(lambda d: guarded(cand_parts, d, lambda: gath_copy(d, d).wait_recv()))
    for k in range(1, half):
        mp_copy(k, mine).start()
    for k in range(1, half):
        mp_copy(k, lax.rem(mine + k, half)).wait_recv()
    for g in range(g_count):
        for j in range(cols):
            for q in range(quarters):
                gstates[g * BS + q * 16 : g * BS + (q + 1) * 16, j * LANES : (j + 1) * LANES] = (
                    gath[g // gper, ((g % gper) * cols + j) * quarters + q]
                )
    gx = gstates[...]
    rows = g_count * BS
    glane = lax.broadcasted_iota(jnp.int32, (rows, LANES), 1)
    glow = glane < HD
    for j in range(pairs):
        cut = slice(j * LANES, (j + 1) * LANES)
        q = dot(gx, weight[0, :, cut]).astype(jnp.bfloat16).astype(jnp.float32) * scaling
        k = dot(gx, weight[1, :, cut])
        v = dot(gx, weight[2, :, cut])
        gq[2 * j] = jnp.where(glow, q, 0.0).astype(jnp.bfloat16)
        gq[2 * j + 1] = jnp.where(glow, swap_halves(q), 0.0).astype(jnp.bfloat16)
        gkv[2 * j] = jnp.where(glow, k, swap_halves(v)).astype(jnp.bfloat16)
        gkv[2 * j + 1] = jnp.where(glow, swap_halves(k), v).astype(jnp.bfloat16)

    for h in range(heads):
        keys = jnp.concatenate([kvb[b * heads + h] for b in range(blocks)], axis=0)
        s = dot_t(gq[h], keys)
        high = jnp.max(s, axis=-1, keepdims=True)
        e = jnp.exp(s - high)
        total = jnp.sum(e, axis=-1, keepdims=True)
        e_high = e.astype(jnp.bfloat16)
        e_low = (e - e_high.astype(jnp.float32)).astype(jnp.bfloat16)
        acc = (dot(e_high, keys) + dot(e_low, keys)) * (1.0 / total)
        level = high + jnp.log(total)
        first = level.astype(jnp.bfloat16).astype(jnp.float32)
        second = (level - first).astype(jnp.bfloat16).astype(jnp.float32)
        third = level - first - second
        packed = jnp.where(
            glane < 16,
            first,
            jnp.where(glane < 32, second, jnp.where(glow, third, acc)),
        ).astype(jnp.bfloat16)
        cuts = rows // rows_per
        for c in range(cuts):
            part[(h // 2) * cuts + c, h % 2] = packed[c * rows_per : (c + 1) * rows_per]
    each_peer(lambda d: guarded(part_parts, d, lambda: part_copy(d, me, d).start()))
    serve_some(1, n)

    to_right.wait_recv()
    to_left.wait_recv()
    win[0:heads] = halo_l[...]
    win[heads : heads + blocks * heads] = kvb[...]
    win[heads + blocks * heads :] = halo_r[...]

    near = 3 + g_count
    slot_lane = lax.broadcasted_iota(jnp.int32, (BS, near * BS), 1)

    def near_keys(at, h):
        return jnp.concatenate([win[at + t * heads] for t in range(3)] + [gkv[h]], axis=0)

    def near_step(b, carry):
        first = me * blocks + b
        start = jnp.where(first == 0, BS, 0)
        stop = jnp.where(first == n * blocks - 1, 2 * BS, 3 * BS)
        outside = (slot_lane < start) | ((slot_lane >= stop) & (slot_lane < 3 * BS))
        for h in range(heads):
            at = b * heads + h
            scores[at] = jnp.where(outside, NEGATIVE, dot_t(qpad[at], near_keys(at, h)))
        return carry

    lax.fori_loop(0, blocks, near_step, 0)

    def combine():
        part_in[me] = part[me]
        each_peer(lambda d: part_copy(d, d, me).wait_recv())
        outs = []
        for parity in range(2):

            def level(d):
                piece = part_in[d, parity].astype(jnp.float32)
                return piece, piece[:, 0:1] + piece[:, 16:17] + piece[:, 32:33]

            def top(d, best):
                return jnp.maximum(best, level(d)[1])

            best = lax.fori_loop(1, n, top, level(0)[1])

            def add(d, so_far):
                piece, high = level(d)
                factor = jnp.exp(high - best)
                return so_far[0] + piece * factor, so_far[1] + factor

            zero = (jnp.zeros((rows_per, LANES), jnp.float32), jnp.zeros((rows_per, 1), jnp.float32))
            summed, total = lax.fori_loop(0, n, add, zero)
            outs.append(summed / total)
        plow = lax.broadcasted_iota(jnp.int32, (rows_per, LANES), 1) < HD
        done = jnp.where(plow, swap_halves(outs[0]), outs[1]).astype(jnp.bfloat16)
        gmine[...] = done
        gout[me] = done
        each_peer(lambda d: gout_copy(d, me).start())

    guarded(part_parts, me, combine)

    each_peer(lambda d: rand_copy(d, d).wait_recv())

    def block_step(b, carry):
        for j in range(pairs):
            halves = []
            for h in (2 * j, 2 * j + 1):
                at = b * heads + h
                early_keys = near_keys(at, h)
                keys = jnp.concatenate([rr[slot[at * R + r]] for r in range(R)], axis=0)
                s = dot_t(qpad[at], keys)
                early_s = scores[at]
                high = jnp.maximum(
                    jnp.max(s, axis=-1, keepdims=True), jnp.max(early_s, axis=-1, keepdims=True)
                )
                e = jnp.exp(s - high)
                early_e = jnp.exp(early_s - high)
                total = jnp.sum(e, axis=-1, keepdims=True) + jnp.sum(
                    early_e, axis=-1, keepdims=True
                )
                share = 1.0 / total
                w = (e * share).astype(jnp.bfloat16)
                early_w = (early_e * share).astype(jnp.bfloat16)
                halves.append(dot(w, keys) + dot(early_w, early_keys))
            att[j, pl.ds(pl.multiple_of(b * BS, BS), BS), :] = jnp.where(
                low, swap_halves(halves[0]), halves[1]
            ).astype(jnp.bfloat16)
        return carry

    lax.fori_loop(0, blocks, block_step, 0)

    each_peer(lambda d: guarded(part_parts, d, lambda: gout_copy(d, d).wait_recv()))
    for j in range(pairs):
        for g in range(g_count):
            cuts = BS // rows_per
            at = (j * g_count + g) * cuts
            row = jnp.concatenate([gout[at + c] for c in range(cuts)], axis=0).astype(jnp.float32)
            for b in range(blocks):
                here = gids[g] == me * blocks + b
                old = att[j, b * BS : (b + 1) * BS, :].astype(jnp.float32)
                att[j, b * BS : (b + 1) * BS, :] = jnp.where(here, row, old).astype(jnp.bfloat16)

    def drain(d):
        tab_copy(d, me).wait_send()
        guarded(cand_parts, d, lambda: cand_copy(d, me, d).wait_send())
        guarded(cand_parts, me, lambda: gath_copy(d, me).wait_send())
        rand_copy(d, me).wait_send()
        guarded(part_parts, d, lambda: part_copy(d, me, d).wait_send())
        guarded(part_parts, me, lambda: gout_copy(d, me).wait_send())

    each_peer(drain)
    for k in range(1, half):
        mp_copy(k, mine).wait_send()
    to_right.wait_send()
    to_left.wait_send()


def tail_kernel(
    chunks,
    att,
    states,
    out_w,
    up_w,
    down_w,
    gain1,
    gain2,
    out,
    mine1,
    theirs1,
    mine2,
    theirs2,
    s1,
    r1,
    s2,
    r2,
    normed,
):
    other = 1 - lax.axis_index("mp")
    barrier = pltpu.get_barrier_semaphore()
    pl.semaphore_signal(barrier, inc=1, device_id={"mp": other}, device_id_type=MESH)
    pl.semaphore_wait(barrier, 1)
    rows = states.shape[0] // chunks

    def swap(mine, theirs, ssem, rsem, c):
        return pltpu.make_async_remote_copy(
            src_ref=mine.at[c],
            dst_ref=theirs.at[c],
            send_sem=ssem.at[c],
            recv_sem=rsem.at[c],
            device_id={"mp": other},
            device_id_type=MESH,
        )

    for c in range(chunks):
        cut = slice(c * rows, (c + 1) * rows)
        acc = dot(att[0, cut, :], out_w[0:LANES, :])
        for j in range(1, att.shape[0]):
            acc = acc + dot(att[j, cut, :], out_w[j * LANES : (j + 1) * LANES, :])
        mine1[c] = acc.astype(mine1.dtype)
        swap(mine1, theirs1, s1, r1, c).start()
    for c in range(chunks):
        cut = slice(c * rows, (c + 1) * rows)
        swap(mine1, theirs1, s1, r1, c).wait_recv()
        summed = mine1[c].astype(jnp.float32) + theirs1[c].astype(jnp.float32)
        norm = layer_norm(states[cut, :].astype(jnp.float32) + summed, gain1[...])
        norm = norm.astype(jnp.bfloat16)
        normed[c] = norm
        v = dot(norm, up_w[...])
        hidden = (v * (1.0 + lax.erf(v * (0.5**0.5))) * 0.5).astype(jnp.bfloat16)
        mine2[c] = dot(hidden, down_w[...]).astype(mine2.dtype)
        swap(mine2, theirs2, s2, r2, c).start()
    for c in range(chunks):
        cut = slice(c * rows, (c + 1) * rows)
        swap(mine2, theirs2, s2, r2, c).wait_recv()
        summed = mine2[c].astype(jnp.float32) + theirs2[c].astype(jnp.float32)
        out[cut, :] = layer_norm(normed[c].astype(jnp.float32) + summed, gain2[...]).astype(
            jnp.bfloat16
        )
    for c in range(chunks):
        swap(mine1, theirs1, s1, r1, c).wait_send()
        swap(mine2, theirs2, s2, r2, c).wait_send()


def vmem_specs(count):
    return [pl.BlockSpec(memory_space=pltpu.VMEM)] * count


def shards(
    states,
    qkv_weight,
    out_weight,
    up_weight,
    down_weight,
    attn_gain,
    mlp_gain,
    global_ids,
    random_owner,
    random_local,
):
    tokens, width = states.shape
    heads = qkv_weight.shape[2] // HD
    pairs = heads // 2
    blocks = tokens // BS
    g_count = global_ids.shape[0]
    n = lax.axis_size("seq")

    owner = random_owner.reshape(-1)
    items = owner.shape[0]
    cap = max(2, items // n + 1)
    head_list = jnp.broadcast_to(
        jnp.arange(heads, dtype=jnp.int32)[None, :, None], (blocks, heads, R)
    ).reshape(-1)
    code = random_local.reshape(-1) * heads + head_list
    earlier = jnp.arange(items)[:, None] > jnp.arange(items)[None, :]
    rank = jnp.sum(((owner[:, None] == owner[None, :]) & earlier).astype(jnp.int32), axis=1)
    slot = owner * cap + rank
    place = owner * LANES + rank
    wanted = jnp.sum(
        jnp.where(
            place[None, None, :]
            == (jnp.arange(n)[:, None] * LANES + jnp.arange(LANES)[None, :])[:, :, None],
            code[None, None, :],
            0,
        ),
        axis=2,
    ).reshape(n, 1, LANES)

    half = lax.axis_size("mp")
    units = (g_count // half) * (width // LANES) * (BS // 16)
    per = -(-units // n)
    part_rows = pairs * g_count * BS
    rows_per = -(-part_rows // n // 16) * 16
    parts = part_rows // rows_per
    bf = jnp.bfloat16
    own = blocks * heads
    dma = pltpu.SemaphoreType.DMA
    att = pl.pallas_call(
        functools.partial(attend_kernel, n, cap, heads, blocks, g_count),
        out_shape=jax.ShapeDtypeStruct((pairs, tokens, LANES), bf),
        in_specs=[pl.BlockSpec(memory_space=pltpu.HBM)] * 2
        + vmem_specs(1)
        + [pl.BlockSpec(memory_space=pltpu.SMEM)] * 2,
        out_specs=pl.BlockSpec(memory_space=pltpu.VMEM),
        scratch_shapes=[
            pltpu.VMEM((tokens, width), bf),
            pltpu.VMEM(qkv_weight.shape, bf),
            pltpu.VMEM((n, 1, LANES), jnp.int32),
            pltpu.SMEM((n, 1, LANES), jnp.int32),
            pltpu.VMEM((units, 16, LANES), bf),
            pltpu.VMEM((n, per, 16, LANES), bf),
            pltpu.VMEM((per, 16, LANES), bf),
            pltpu.VMEM((half, units, 16, LANES), bf),
            pltpu.VMEM((g_count * BS, width), bf),
            pltpu.VMEM((own, BS, LANES), bf),
            pltpu.VMEM((own, BS, LANES), bf),
            pltpu.VMEM((n * cap, BS, LANES), bf),
            pltpu.VMEM((n * cap, BS, LANES), bf),
            pltpu.VMEM((heads, BS, LANES), bf),
            pltpu.VMEM((heads, BS, LANES), bf),
            pltpu.VMEM((own + 2 * heads, BS, LANES), bf),
            pltpu.VMEM((heads, g_count * BS, LANES), bf),
            pltpu.VMEM((heads, g_count * BS, LANES), bf),
            pltpu.VMEM((parts, 2, rows_per, LANES), bf),
            pltpu.VMEM((n, 2, rows_per, LANES), bf),
            pltpu.VMEM((rows_per, LANES), bf),
            pltpu.VMEM((parts, rows_per, LANES), bf),
            pltpu.VMEM((own, BS, (3 + g_count) * BS), jnp.float32),
        ]
        + [dma((n,))] * 8
        + [dma((2,))] * 2
        + [dma((n,))] * 4
        + [dma((half,))] * 2
        + [dma(()), dma((4,))],
        cost_estimate=pl.CostEstimate(
            flops=30_000_000_000, bytes_accessed=20_000_000, transcendentals=0
        ),
        compiler_params=pltpu.CompilerParams(
            collective_id=0, has_side_effects=True, vmem_limit_bytes=32 * 1024 * 1024
        ),
    )(
        pltpu.with_memory_space_constraint(states, pltpu.HBM),
        pltpu.with_memory_space_constraint(qkv_weight, pltpu.HBM),
        wanted,
        slot,
        global_ids,
    )

    chunks = 4
    rows = tokens // chunks
    link = jnp.bfloat16
    return pl.pallas_call(
        functools.partial(tail_kernel, chunks),
        out_shape=jax.ShapeDtypeStruct((tokens, width), bf),
        in_specs=vmem_specs(7),
        out_specs=pl.BlockSpec(memory_space=pltpu.VMEM),
        scratch_shapes=[pltpu.VMEM((chunks, rows, width), link)] * 4
        + [dma((chunks,))] * 4
        + [pltpu.VMEM((chunks, rows, width), bf)],
        compiler_params=pltpu.CompilerParams(
            collective_id=1, has_side_effects=True, vmem_limit_bytes=32 * 1024 * 1024
        ),
    )(
        att,
        states,
        out_weight,
        up_weight,
        down_weight,
        attn_gain.reshape(1, width),
        mlp_gain.reshape(1, width),
    )


def solution(mesh):
    in_specs = (
        P("seq", None),
        P(None, None, "mp"),
        P("mp", None),
        P(None, "mp"),
        P("mp", None),
        P(),
        P(),
        P(),
        P("mp", "seq", None, None),
        P("mp", "seq", None, None),
    )
    out_specs = P("seq", None)
    return jax.shard_map(shards, mesh=mesh, in_specs=in_specs, out_specs=out_specs, check_vma=False)
```

profile of v0, /device:TPU:15, one launch (start us, length us, event | category | flops | bytes accessed | tf_op | source)
XLA Modules:
  0.0 77.9 jit_solution(16122870020571309998)
XLA Ops:
  0.0 0.7 reshape.66.gain1
  0.7 0.7 reshape.67.gain2
  1.4 0.7 broadcast_multiply_fusion
  2.1 0.1 iota_add_fusion
  2.1 0.1 copy.16
  2.3 0.1 mul.42
  2.4 0.8 %copy.15 = s32[1,4,6,3]{3,2,1,0:T(8,128)S(1)} copy(s32[1,4,6,3]{2,1,3,0:T(4,128)} %param.18) | data formatting | bytes 576 | tf_op args[8]
  3.2 0.1 reshape.63
  3.3 0.2 convert_reduce_fusion
  3.5 0.1 reshape.64
  3.6 0.1 select_reduce_fusion
  3.7 0.0 copy-start.4
  3.7 0.6 copy-done.4
  4.4 0.0 copy-start
  4.4 0.0 copy-start.1
  4.4 0.0 copy-start.2
  4.4 0.0 copy-start.3
  4.4 65.2 %shard_map.100.att = bf16[3,256,128]{2,1,0:T(8,128)(2,1)S(1)} custom-call(bf16[256,768]{1,0:T(8,128)(2,1)} %states.1, bf16[3,768,384]{2,1,0:T(8,128)(2,1)} %weight_hbm.1, s32[16,1,128]{2,1,0:T(1,128)S(1)} %bitcast.1, s32[72]{0:T(128)S(1)} %get-tuple-element.5.slot, s32[2]{0:T(128)S(1)} %copy-done.4), custom_call_target="tpu_custom_call" | custom-call | flops 30000001024 | bytes 20000000 | tf_op jit(solution)/shard_map/pallas_call | solution.py:556
  69.6 0.0 copy-done
  69.6 0.0 copy-done.1
  69.6 0.0 copy-done.2
  69.6 0.0 copy-done.3
  69.6 7.5 %shard_map.101 = bf16[256,768]{1,0:T(8,128)(2,1)S(1)} custom-call(bf16[3,256,128]{2,1,0:T(8,128)(2,1)S(1)} %shard_map.100.att, bf16[256,768]{1,0:T(8,128)(2,1)S(1)} %copy-done.3, bf16[384,768]{1,0:T(8,128)(2,1)S(1)} %copy-done.2, bf16[768,1536]{1,0:T(8,128)(2,1)S(1)} %copy-done, bf16[1536,768]{1,0:T(8,128)(2,1)S(1)} %copy-done.1, ...), custom_call_target="tpu_custom_call" | custom-call | tf_op jit(solution)/shard_map/pallas_call | solution.py:610
  77.1 0.7 copy.18
  (4 shorter events, 0.0 us)
Async XLA Ops:
  3.7 0.7 copy-start.4
  4.4 65.2 %copy-start = (bf16[768,1536]{1,0:T(8,128)(2,1)S(1)}, bf16[768,1536]{1,0:T(8,128)(2,1)}, u32[]{:S(2)}) copy-start(bf16[768,1536]{1,0:T(8,128)(2,1)} %up_w.1) | copy-start | bytes 7077892
  4.4 65.2 %copy-start.1 = (bf16[1536,768]{1,0:T(8,128)(2,1)S(1)}, bf16[1536,768]{1,0:T(8,128)(2,1)}, u32[]{:S(2)}) copy-start(bf16[1536,768]{1,0:T(8,128)(2,1)} %down_w.1) | copy-start | bytes 7077892
  4.4 65.2 %copy-start.2 = (bf16[384,768]{1,0:T(8,128)(2,1)S(1)}, bf16[384,768]{1,0:T(8,128)(2,1)}, u32[]{:S(2)}) copy-start(bf16[384,768]{1,0:T(8,128)(2,1)} %out_w.1) | copy-start | bytes 1769476
  4.4 65.2 %copy-start.3 = (bf16[256,768]{1,0:T(8,128)(2,1)S(1)}, bf16[256,768]{1,0:T(8,128)(2,1)}, u32[]{:S(2)}) copy-start(bf16[256,768]{1,0:T(8,128)(2,1)} %states.1) | copy-start | bytes 1179652
where the time goes:
time: 78.2 us; the launch traced here: 77.9 us
  Pallas kernels  72.7 us (93%)
  local copies, waits for them, and re-layouts  3.99 us (5%)
  other arithmetic  1.09 us (1%)
    pallas_call x1, Pallas kernels, shards(): pl.pallas_call(functools.partial(attend_kernel, n, cap, heads, blocks, g_...  65.2 us
    pallas_call x1, Pallas kernels, shards(): pl.pallas_call(functools.partial(tail_kernel, chunks), out_shape=jax.Shap...  7.51 us
    unnamed x12, local copies, waits for them, and re-layouts  2.21 us

commit v1 on v0

--- a/solution.py
+++ b/solution.py
@@ -434,6 +434,326 @@
     to_left.wait_send()
 
 
+TREES = ("zxy", "zyx", "yzx", "xzy")
+PLACES = ((0, 0), (1, 0), (0, 1), (1, 1))
+TURNS = (
+    (-8.5, -3.0, -1.5, 10.5),
+    (-5.5, 3.0, 0.0, 8.0),
+    (-2.0, 5.0, 3.5, 13.5),
+    (-1.5, 2.0, 7.5, 11.0),
+)
+LAG = 3
+
+
+def arrivals(depth):
+    pieces = [
+        (3.5 * slot + TURNS[t][p], t, slot, *PLACES[p])
+        for t in range(len(TREES))
+        for slot in range(depth)
+        for p in range(len(PLACES))
+        if slot or p
+    ]
+    return [piece[1:] for piece in sorted(pieces)]
+
+
+def hops(tree, slot, dx, dy):
+    moved = {"x": dx, "y": dy, "z": slot}
+    last = max((i for i in range(3) if moved[tree[i]]), default=-1)
+    onward = tree[last + 1 :]
+    via = tree[last] if last >= 0 else ""
+    return via, ("z" if via == "z" else "") + onward
+
+
+def slots(z, depth):
+    inward = 1 if 2 * z < depth else -1
+    return sorted(range(depth), key=lambda q: (abs(q - z), (z - q) * inward))
+
+
+def gather_kernel(
+    n,
+    heads,
+    blocks,
+    g_count,
+    states_hbm,
+    weight_hbm,
+    owner,
+    local,
+    gids,
+    att,
+    xs,
+    wq,
+    wkv,
+    kv,
+    q_all,
+    wide,
+    gmine,
+    gout,
+    scores,
+    s_x,
+    s_y,
+    s_up,
+    s_down,
+    s_mp,
+    r_ici,
+    r_mp,
+    s_gout,
+    r_gout,
+    l_sem,
+):
+    me = lax.axis_index("seq")
+    mine = lax.axis_index("mp")
+    pairs = heads // 2
+    inner = heads * HD
+    trees = len(TREES)
+    per = 2 * trees
+    piece = xs.shape[1]
+    width = xs.shape[2]
+    tokens = per * piece
+    depth = n // 4
+    units = pairs * g_count
+    x_at, y_at, z_at = lax.rem(me, 2), lax.rem(me // 2, 2), me // 4
+
+    def remote(src, dst, ssem, rsem, where):
+        return pltpu.make_async_remote_copy(
+            src_ref=src,
+            dst_ref=dst,
+            send_sem=ssem,
+            recv_sem=rsem,
+            device_id=where,
+            device_id_type=MESH,
+        )
+
+    def peer(k):
+        return lax.rem(me + k, n)
+
+    def each_peer(body):
+        def step(k, carry):
+            body(peer(k))
+            return carry
+
+        lax.fori_loop(1, n, step, 0)
+
+    def plane(slot):
+        if slot == 0:
+            return z_at
+        found = slots(0, depth)[slot]
+        for z in range(1, depth):
+            found = jnp.where(z_at == z, slots(z, depth)[slot], found)
+        return found
+
+    def shard_of(slot, dx, dy):
+        x = 1 - x_at if dx else x_at
+        y = 1 - y_at if dy else y_at
+        return plane(slot) * 4 + y * 2 + x
+
+    def ici(shard, t, ssem, d):
+        at = xs.at[(shard * 2 + mine) * trees + t]
+        return remote(at, at, ssem.at[shard * trees + t], r_ici.at[shard * trees + t], {"seq": d})
+
+    def across(shard, t, core):
+        at = xs.at[(shard * 2 + core) * trees + t]
+        return remote(
+            at, at, s_mp.at[shard * trees + t], r_mp.at[shard * trees + t], {"mp": 1 - mine}
+        )
+
+    x_peer = me + 1 - 2 * x_at
+    y_peer = me + 2 - 4 * y_at
+    up, down = lax.rem(me + 4, n), lax.rem(me + n - 4, n)
+
+    def onward(t, slot, dx, dy, act):
+        shard = shard_of(slot, dx, dy)
+        via, axes = hops(TREES[t], slot, dx, dy)
+        for axis in axes:
+            if axis == "x":
+                act(ici(shard, t, s_x, x_peer))
+            elif axis == "y":
+                act(ici(shard, t, s_y, y_peer))
+            else:
+                source = plane(slot)
+                go_up = z_at < depth - 1
+                go_down = z_at > 0
+                if via == "z":
+                    go_up = go_up & (source < z_at)
+                    go_down = go_down & (source > z_at)
+                pl.when(go_up)(lambda: act(ici(shard, t, s_up, up)))
+                pl.when(go_down)(lambda: act(ici(shard, t, s_down, down)))
+        if slot or dx or dy:
+            act(across(shard, t, mine))
+
+    order = arrivals(depth)
+
+    loads = [
+        pltpu.make_async_copy(states_hbm, xs.at[pl.ds(me * per, per)], l_sem.at[0]),
+        pltpu.make_async_copy(weight_hbm.at[1], wkv.at[:, 0:inner], l_sem.at[1]),
+        pltpu.make_async_copy(weight_hbm.at[2], wkv.at[:, inner : 2 * inner], l_sem.at[2]),
+        pltpu.make_async_copy(weight_hbm.at[0], wq, l_sem.at[3]),
+    ]
+    for load in loads:
+        load.start()
+    barrier = pltpu.get_barrier_semaphore()
+    each_peer(
+        lambda d: pl.semaphore_signal(barrier, inc=1, device_id={"seq": d}, device_id_type=MESH)
+    )
+    pl.semaphore_signal(barrier, inc=1, device_id={"mp": 1 - mine}, device_id_type=MESH)
+    loads[0].wait()
+    pl.semaphore_wait(barrier, n)
+    for t in range(trees):
+        onward(t, 0, 0, 0, lambda copy: copy.start())
+    for load in loads[1:]:
+        load.wait()
+
+    def project(shard):
+        def step(c, carry):
+            x = xs[pl.ds(shard * per, per)].reshape(tokens, width)
+            cut = pl.ds(pl.multiple_of(c * 256, 256), 256)
+            y = dot(x, wkv[:, cut]).astype(jnp.bfloat16)
+            kv[pl.ds(shard * blocks, blocks), :, cut] = y.reshape(blocks, BS, 256)
+            return carry
+
+        lax.fori_loop(0, 2 * inner // 256, step, 0)
+
+    x = xs[pl.ds(me * per, per)].reshape(tokens, width)
+    scaling = HD ** (-0.5)
+    q_all[...] = (
+        dot(x, wq[...]).astype(jnp.bfloat16).astype(jnp.float32) * scaling
+    ).astype(jnp.bfloat16)
+    project(me)
+
+    waiting = []
+    left = dict()
+
+    def finish(place):
+        shard = shard_of(*place)
+        for t in range(trees):
+            across(shard, t, 1 - mine).wait_recv()
+        project(shard)
+
+    for t, slot, dx, dy in order:
+        shard = shard_of(slot, dx, dy)
+        ici(shard, t, s_x, x_peer).wait_recv()
+        onward(t, slot, dx, dy, lambda copy: copy.start())
+        waiting = [(count - 1, place) for count, place in waiting]
+        while waiting and waiting[0][0] <= 0:
+            finish(waiting.pop(0)[1])
+        place = (slot, dx, dy)
+        left[place] = left.get(place, trees) - 1
+        if left[place] == 0:
+            waiting.append((LAG, place))
+    for _, place in waiting:
+        finish(place)
+
+    lane = lax.broadcasted_iota(jnp.int32, (BS, LANES), 1)
+    low = lane < HD
+
+    def split(q):
+        zero = jnp.zeros_like(q)
+        return jnp.concatenate([jnp.where(low, q, zero), jnp.where(low, zero, q)], axis=0)
+
+    def together(out):
+        return jnp.where(low, out[0:BS], out[BS : 2 * BS]).astype(jnp.bfloat16)
+
+    chunk = wide.shape[2]
+    per_chunk = chunk // BS
+    chunks = wide.shape[0]
+
+    def share():
+        j, g = me // g_count, lax.rem(me, g_count)
+        k_cut = pl.ds(pl.multiple_of(j * LANES, LANES), LANES)
+        v_cut = pl.ds(pl.multiple_of(inner + j * LANES, LANES), LANES)
+        rows = BS // piece
+        x = xs[pl.ds(gids[g] * rows, rows)].reshape(BS, width)
+        q = dot(x, wq[:, k_cut]).astype(jnp.bfloat16).astype(jnp.float32) * scaling
+        q2 = split(q.astype(jnp.bfloat16))
+
+        def score(c, best):
+            keys = kv[pl.ds(c * per_chunk, per_chunk), :, k_cut].reshape(chunk, LANES)
+            s = dot_t(q2, keys)
+            wide[c] = s
+            return jnp.maximum(best, jnp.max(s, axis=-1, keepdims=True))
+
+        high = lax.fori_loop(0, chunks, score, jnp.full((2 * BS, 1), NEGATIVE, jnp.float32))
+
+        def add(c, so_far):
+            values = kv[pl.ds(c * per_chunk, per_chunk), :, v_cut].reshape(chunk, LANES)
+            e = jnp.exp(wide[c] - high)
+            e_high = e.astype(jnp.bfloat16)
+            e_low = (e - e_high.astype(jnp.float32)).astype(jnp.bfloat16)
+            return (
+                so_far[0] + dot(e_high, values) + dot(e_low, values),
+                so_far[1] + jnp.sum(e, axis=-1, keepdims=True),
+            )
+
+        zero = (jnp.zeros((2 * BS, LANES), jnp.float32), jnp.zeros((2 * BS, 1), jnp.float32))
+        summed, total = lax.fori_loop(0, chunks, add, zero)
+        done = together(summed / total)
+        gmine[...] = done
+        gout[me] = done
+        each_peer(lambda d: gout_copy(d, me).start())
+
+    def gout_copy(d, unit):
+        return remote(gmine, gout.at[unit], s_gout.at[d], r_gout.at[unit], {"seq": d})
+
+    def guarded(who, body):
+        if units < n:
+            pl.when(who < units)(body)
+        else:
+            body()
+
+    guarded(me, share)
+
+    slot_lane = lax.broadcasted_iota(jnp.int32, (1, 3 * BS), 1)
+    last = n * blocks - 1
+
+    def block_step(b, carry):
+        first = me * blocks + b
+        start = jnp.where(first == 0, BS, 0)
+        stop = jnp.where(first == last, 2 * BS, 3 * BS)
+        bias = jnp.where((slot_lane < start) | (slot_lane >= stop), NEGATIVE, 0.0)
+        near = [jnp.maximum(first - 1, 0), first, jnp.minimum(first + 1, last)]
+        ends = [gids[g] for g in range(g_count)]
+        for j in range(pairs):
+            one = [
+                owner[0, b, 2 * j, r] * blocks + local[0, b, 2 * j, r] for r in range(R)
+            ]
+            two = [
+                owner[0, b, 2 * j + 1, r] * blocks + local[0, b, 2 * j + 1, r] for r in range(R)
+            ]
+
+            def rows(base):
+                cut = slice(base + j * LANES, base + (j + 1) * LANES)
+                return jnp.concatenate(
+                    [kv[at, :, cut] for at in near]
+                    + [jnp.where(low, kv[a, :, cut], kv[c, :, cut]) for a, c in zip(one, two)]
+                    + [kv[at, :, cut] for at in ends],
+                    axis=0,
+                )
+
+            q = q_all[pl.ds(pl.multiple_of(b * BS, BS), BS), j * LANES : (j + 1) * LANES]
+            s = dot_t(split(q), rows(0))
+            s = jnp.concatenate([s[:, 0 : 3 * BS] + bias, s[:, 3 * BS :]], axis=1)
+            e = jnp.exp(s - jnp.max(s, axis=-1, keepdims=True))
+            w = (e * (1.0 / jnp.sum(e, axis=-1, keepdims=True))).astype(jnp.bfloat16)
+            att[j, pl.ds(pl.multiple_of(b * BS, BS), BS), :] = together(dot(w, rows(inner)))
+        return carry
+
+    lax.fori_loop(0, blocks, block_step, 0)
+
+    each_peer(lambda d: guarded(d, lambda: gout_copy(d, d).wait_recv()))
+    for j in range(pairs):
+        for g in range(g_count):
+            row = gout[j * g_count + g].astype(jnp.float32)
+            for b in range(blocks):
+                here = gids[g] == me * blocks + b
+                old = att[j, b * BS : (b + 1) * BS, :].astype(jnp.float32)
+                att[j, b * BS : (b + 1) * BS, :] = jnp.where(here, row, old).astype(jnp.bfloat16)
+
+    for t in range(trees):
+        onward(t, 0, 0, 0, lambda copy: copy.wait_send())
+    for t, slot, dx, dy in order:
+        onward(t, slot, dx, dy, lambda copy: copy.wait_send())
+    each_peer(lambda d: guarded(me, lambda: gout_copy(d, me).wait_send()))
+
+
 def tail_kernel(
     chunks,
     att,
@@ -504,18 +824,7 @@
     return [pl.BlockSpec(memory_space=pltpu.VMEM)] * count
 
 
-def shards(
-    states,
-    qkv_weight,
-    out_weight,
-    up_weight,
-    down_weight,
-    attn_gain,
-    mlp_gain,
-    global_ids,
-    random_owner,
-    random_local,
-):
+def attend_requested(states, qkv_weight, global_ids, random_owner, random_local):
     tokens, width = states.shape
     heads = qkv_weight.shape[2] // HD
     pairs = heads // 2
@@ -553,7 +862,7 @@
     bf = jnp.bfloat16
     own = blocks * heads
     dma = pltpu.SemaphoreType.DMA
-    att = pl.pallas_call(
+    return pl.pallas_call(
         functools.partial(attend_kernel, n, cap, heads, blocks, g_count),
         out_shape=jax.ShapeDtypeStruct((pairs, tokens, LANES), bf),
         in_specs=[pl.BlockSpec(memory_space=pltpu.HBM)] * 2
@@ -604,6 +913,90 @@
         global_ids,
     )
 
+
+def attend_gathered(states, qkv_weight, global_ids, random_owner, random_local):
+    tokens, width = states.shape
+    inner = qkv_weight.shape[2]
+    heads = inner // HD
+    pairs = heads // 2
+    blocks = tokens // BS
+    g_count = global_ids.shape[0]
+    n = lax.axis_size("seq")
+    trees = len(TREES)
+    piece = tokens // (2 * trees)
+    chunk = 8 * BS
+    bf = jnp.bfloat16
+    dma = pltpu.SemaphoreType.DMA
+    return pl.pallas_call(
+        functools.partial(gather_kernel, n, heads, blocks, g_count),
+        out_shape=jax.ShapeDtypeStruct((pairs, tokens, LANES), bf),
+        in_specs=[pl.BlockSpec(memory_space=pltpu.HBM)] * 2
+        + [pl.BlockSpec(memory_space=pltpu.SMEM)] * 3,
+        out_specs=pl.BlockSpec(memory_space=pltpu.VMEM),
+        scratch_shapes=[
+            pltpu.VMEM((n * 2 * trees, piece, width), bf),
+            pltpu.VMEM((width, inner), bf),
+            pltpu.VMEM((width, 2 * inner), bf),
+            pltpu.VMEM((n * blocks, BS, 2 * inner), bf),
+            pltpu.VMEM((tokens, inner), bf),
+            pltpu.VMEM((n * tokens // chunk, 2 * BS, chunk), jnp.float32),
+            pltpu.VMEM((BS, LANES), bf),
+            pltpu.VMEM((pairs * g_count, BS, LANES), bf),
+            pltpu.VMEM((8, LANES), jnp.float32),
+        ]
+        + [dma((n * trees,))] * 7
+        + [dma((n,)), dma((pairs * g_count,)), dma((4,))],
+        cost_estimate=pl.CostEstimate(
+            flops=30_000_000_000, bytes_accessed=20_000_000, transcendentals=0
+        ),
+        compiler_params=pltpu.CompilerParams(
+            collective_id=0, has_side_effects=True, vmem_limit_bytes=40 * 1024 * 1024
+        ),
+    )(
+        pltpu.with_memory_space_constraint(
+            states.reshape(2 * trees, piece, width), pltpu.HBM
+        ),
+        pltpu.with_memory_space_constraint(qkv_weight, pltpu.HBM),
+        random_owner,
+        random_local,
+        global_ids,
+    )
+
+
+def gathers(states, qkv_weight, global_ids):
+    tokens, width = states.shape
+    n = lax.axis_size("seq")
+    inner = qkv_weight.shape[2]
+    held = n * tokens * (width + 2 * inner) * 2
+    units = inner // LANES * global_ids.shape[0]
+    return (
+        n % 4 == 0
+        and lax.axis_size("mp") == 2
+        and held <= 24 * 1024 * 1024
+        and units <= n
+        and tokens % (2 * len(TREES) * 16) == 0
+        and 2 * inner % 256 == 0
+    )
+
+
+def shards(
+    states,
+    qkv_weight,
+    out_weight,
+    up_weight,
+    down_weight,
+    attn_gain,
+    mlp_gain,
+    global_ids,
+    random_owner,
+    random_local,
+):
+    tokens, width = states.shape
+    bf = jnp.bfloat16
+    dma = pltpu.SemaphoreType.DMA
+    attend = attend_gathered if gathers(states, qkv_weight, global_ids) else attend_requested
+    att = attend(states, qkv_weight, global_ids, random_owner, random_local)
+
     chunks = 4
     rows = tokens // chunks
     link = jnp.bfloat16

time: 78.2 us -> 67.2 us (0.86)
  the two profiles are of different devices: /device:TPU:15 before, /device:TPU:0 now
where the time goes in v1:
time: 67.2 us; the launch traced here: 66.9 us
  Pallas kernels  62.4 us (93%)
  local copies, waits for them, and re-layouts  4.39 us (7%)
    pallas_call x1, Pallas kernels, attend_gathered(): pl.pallas_call(functools.partial(gather_kernel, n, heads, blocks, g_count...  54.6 us
    pallas_call x1, Pallas kernels, shards(): pl.pallas_call(functools.partial(tail_kernel, chunks), out_shape=jax.Shap...  7.83 us
    unnamed x13, local copies, waits for them, and re-layouts  3.01 us

profile of v1, /device:TPU:0, one launch (start us, length us, event | category | flops | bytes accessed | tf_op | source)
XLA Modules:
  0.0 66.9 jit_solution(4829602770890913600)
XLA Ops:
  0.0 0.7 %reshape.10.gain1 = f32[1,768]{1,0:T(1,128)S(1)} reshape(f32[768]{0:T(1024)} %param.15) | data formatting | bytes 6144 | tf_op jit(solution)/shard_map/reshape | solution.py:1020
  0.7 0.7 %reshape.11.gain2 = f32[1,768]{1,0:T(1,128)S(1)} reshape(f32[768]{0:T(1024)} %param.16) | data formatting | bytes 6144 | tf_op jit(solution)/shard_map/reshape | solution.py:1021
  1.4 0.8 %copy.11.owner = s32[1,4,6,3]{3,2,1,0:T(8,128)S(1)} copy(s32[1,4,6,3]{2,1,3,0:T(4,128)} %param.18) | data formatting | bytes 576 | tf_op args[8]
  2.2 0.8 %copy.12.local = s32[1,4,6,3]{3,2,1,0:T(8,128)S(1)} copy(s32[1,4,6,3]{2,1,3,0:T(4,128)} %param.19) | data formatting | bytes 576 | tf_op args[9]
  3.0 0.0 copy-start.4
  3.0 0.7 copy-done.4
  3.6 0.0 copy-start
  3.6 0.0 copy-start.1
  3.6 0.0 copy-start.2
  3.6 0.0 copy-start.3
  3.6 54.6 %shard_map.100.att = bf16[3,256,128]{2,1,0:T(8,128)(2,1)S(1)} custom-call(bf16[8,32,768]{2,1,0:T(8,128)(2,1)} %bitcast.1, bf16[3,768,384]{2,1,0:T(8,128)(2,1)} %weight_hbm.1, s32[1,4,6,3]{3,2,1,0:T(8,128)S(1)} %copy.11.owner, s32[1,4,6,3]{3,2,1,0:T(8,128)S(1)} %copy.12.local, s32[2]{0:T(128)S(1)} %copy-done.4), custom_call_target="tpu_custom_call" | custom-call | flops 30000001024 | bytes 20000000 | tf_op jit(solution)/shard_map/pallas_call | solution.py:930
  58.2 0.0 copy-done
  58.3 0.0 copy-done.1
  58.3 0.0 copy-done.2
  58.3 0.0 copy-done.3
  58.3 7.8 %shard_map.101 = bf16[256,768]{1,0:T(8,128)(2,1)S(1)} custom-call(bf16[3,256,128]{2,1,0:T(8,128)(2,1)S(1)} %shard_map.100.att, bf16[256,768]{1,0:T(8,128)(2,1)S(1)} %copy-done.3, bf16[384,768]{1,0:T(8,128)(2,1)S(1)} %copy-done.2, bf16[768,1536]{1,0:T(8,128)(2,1)S(1)} %copy-done, bf16[1536,768]{1,0:T(8,128)(2,1)S(1)} %copy-done.1, ...), custom_call_target="tpu_custom_call" | custom-call | tf_op jit(solution)/shard_map/pallas_call | solution.py:1003
  66.1 0.7 %copy.14 = bf16[256,768]{1,0:T(8,128)(2,1)} copy(bf16[256,768]{1,0:T(8,128)(2,1)S(1)} %shard_map.101) | data formatting | bytes 786432
Async XLA Ops:
  3.0 0.7 copy-start.4
  3.6 54.6 %copy-start = (bf16[768,1536]{1,0:T(8,128)(2,1)S(1)}, bf16[768,1536]{1,0:T(8,128)(2,1)}, u32[]{:S(2)}) copy-start(bf16[768,1536]{1,0:T(8,128)(2,1)} %up_w.1) | copy-start | bytes 7077892
  3.6 54.6 %copy-start.1 = (bf16[1536,768]{1,0:T(8,128)(2,1)S(1)}, bf16[1536,768]{1,0:T(8,128)(2,1)}, u32[]{:S(2)}) copy-start(bf16[1536,768]{1,0:T(8,128)(2,1)} %down_w.1) | copy-start | bytes 7077892
  3.6 54.6 %copy-start.2 = (bf16[384,768]{1,0:T(8,128)(2,1)S(1)}, bf16[384,768]{1,0:T(8,128)(2,1)}, u32[]{:S(2)}) copy-start(bf16[384,768]{1,0:T(8,128)(2,1)} %out_w.1) | copy-start | bytes 1769476
  3.6 54.6 %copy-start.3 = (bf16[256,768]{1,0:T(8,128)(2,1)S(1)}, bf16[256,768]{1,0:T(8,128)(2,1)}, u32[]{:S(2)}) copy-start(bf16[256,768]{1,0:T(8,128)(2,1)} %states.1) | copy-start | bytes 1179652

commit v2 on v1

--- a/solution.py
+++ b/solution.py
@@ -443,6 +443,7 @@
     (-1.5, 2.0, 7.5, 11.0),
 )
 LAG = 3
+CHUNKS = 2
 
 
 def arrivals(depth):
@@ -474,12 +475,18 @@
     heads,
     blocks,
     g_count,
+    chunks,
     states_hbm,
     weight_hbm,
-    owner,
-    local,
-    gids,
-    att,
+    owner_hbm,
+    local_hbm,
+    gids_hbm,
+    out_hbm,
+    up_hbm,
+    down_hbm,
+    gain1_hbm,
+    gain2_hbm,
+    out,
     xs,
     wq,
     wkv,
@@ -488,7 +495,20 @@
     wide,
     gmine,
     gout,
-    scores,
+    owner,
+    local,
+    gids,
+    att,
+    out_w,
+    up_w,
+    down_w,
+    gain1,
+    gain2,
+    mine1,
+    theirs1,
+    mine2,
+    theirs2,
+    normed,
     s_x,
     s_y,
     s_up,
@@ -498,6 +518,10 @@
     r_mp,
     s_gout,
     r_gout,
+    s1,
+    r1,
+    s2,
+    r2,
     l_sem,
 ):
     me = lax.axis_index("seq")
@@ -582,35 +606,46 @@
 
     order = arrivals(depth)
 
-    loads = [
-        pltpu.make_async_copy(states_hbm, xs.at[pl.ds(me * per, per)], l_sem.at[0]),
-        pltpu.make_async_copy(weight_hbm.at[1], wkv.at[:, 0:inner], l_sem.at[1]),
-        pltpu.make_async_copy(weight_hbm.at[2], wkv.at[:, inner : 2 * inner], l_sem.at[2]),
-        pltpu.make_async_copy(weight_hbm.at[0], wq, l_sem.at[3]),
+    pairs_of = [
+        (states_hbm, xs.at[pl.ds(me * per, per)]),
+        (weight_hbm.at[1], wkv.at[:, 0:inner]),
+        (weight_hbm.at[2], wkv.at[:, inner : 2 * inner]),
+        (weight_hbm.at[0], wq),
+        (owner_hbm, owner),
+        (local_hbm, local),
+        (gids_hbm, gids),
+        (gain1_hbm, gain1),
+        (gain2_hbm, gain2),
+        (out_hbm, out_w),
+        (up_hbm, up_w),
+        (down_hbm, down_w),
     ]
-    for load in loads:
+    loads = [pltpu.make_async_copy(a, b, l_sem.at[i]) for i, (a, b) in enumerate(pairs_of)]
+    loads[0].start()
+    barrier = pltpu.get_barrier_semaphore()
+    for d in (x_peer, y_peer):
+        pl.semaphore_signal(barrier, inc=1, device_id={"seq": d}, device_id_type=MESH)
+    pl.semaphore_signal(barrier, inc=1, device_id={"mp": 1 - mine}, device_id_type=MESH)
+    for there, d in ((z_at < depth - 1, up), (z_at > 0, down)):
+        pl.when(there)(
+            lambda d=d: pl.semaphore_signal(
+                barrier, inc=1, device_id={"seq": d}, device_id_type=MESH
+            )
+        )
+    for load in loads[1:]:
         load.start()
-    barrier = pltpu.get_barrier_semaphore()
-    each_peer(
-        lambda d: pl.semaphore_signal(barrier, inc=1, device_id={"seq": d}, device_id_type=MESH)
-    )
-    pl.semaphore_signal(barrier, inc=1, device_id={"mp": 1 - mine}, device_id_type=MESH)
+    column = jnp.where(z_at < depth - 1, 1, 0) + jnp.where(z_at > 0, 1, 0)
     loads[0].wait()
-    pl.semaphore_wait(barrier, n)
+    pl.semaphore_wait(barrier, 3 + column)
     for t in range(trees):
         onward(t, 0, 0, 0, lambda copy: copy.start())
-    for load in loads[1:]:
+    for load in loads[1:4]:
         load.wait()
 
     def project(shard):
-        def step(c, carry):
-            x = xs[pl.ds(shard * per, per)].reshape(tokens, width)
-            cut = pl.ds(pl.multiple_of(c * 256, 256), 256)
-            y = dot(x, wkv[:, cut]).astype(jnp.bfloat16)
-            kv[pl.ds(shard * blocks, blocks), :, cut] = y.reshape(blocks, BS, 256)
-            return carry
-
-        lax.fori_loop(0, 2 * inner // 256, step, 0)
+        x = xs[pl.ds(shard * per, per)].reshape(tokens, width)
+        y = dot(x, wkv[...]).astype(jnp.bfloat16)
+        kv[pl.ds(shard * blocks, blocks)] = y.reshape(blocks, BS, 2 * inner)
 
     x = xs[pl.ds(me * per, per)].reshape(tokens, width)
     scaling = HD ** (-0.5)
@@ -641,6 +676,8 @@
             waiting.append((LAG, place))
     for _, place in waiting:
         finish(place)
+    for load in loads[4:]:
+        load.wait()
 
     lane = lax.broadcasted_iota(jnp.int32, (BS, LANES), 1)
     low = lane < HD
@@ -654,7 +691,7 @@
 
     chunk = wide.shape[2]
     per_chunk = chunk // BS
-    chunks = wide.shape[0]
+    steps = wide.shape[0]
 
     def share():
         j, g = me // g_count, lax.rem(me, g_count)
@@ -671,7 +708,7 @@
             wide[c] = s
             return jnp.maximum(best, jnp.max(s, axis=-1, keepdims=True))
 
-        high = lax.fori_loop(0, chunks, score, jnp.full((2 * BS, 1), NEGATIVE, jnp.float32))
+        high = lax.fori_loop(0, steps, score, jnp.full((2 * BS, 1), NEGATIVE, jnp.float32))
 
         def add(c, so_far):
             values = kv[pl.ds(c * per_chunk, per_chunk), :, v_cut].reshape(chunk, LANES)
@@ -684,7 +721,7 @@
             )
 
         zero = (jnp.zeros((2 * BS, LANES), jnp.float32), jnp.zeros((2 * BS, 1), jnp.float32))
-        summed, total = lax.fori_loop(0, chunks, add, zero)
+        summed, total = lax.fori_loop(0, steps, add, zero)
         done = together(summed / total)
         gmine[...] = done
         gout[me] = done
@@ -713,10 +750,10 @@
         ends = [gids[g] for g in range(g_count)]
         for j in range(pairs):
             one = [
-                owner[0, b, 2 * j, r] * blocks + local[0, b, 2 * j, r] for r in range(R)
+                owner[0, r, b, 2 * j] * blocks + local[0, r, b, 2 * j] for r in range(R)
             ]
             two = [
-                owner[0, b, 2 * j + 1, r] * blocks + local[0, b, 2 * j + 1, r] for r in range(R)
+                owner[0, r, b, 2 * j + 1] * blocks + local[0, r, b, 2 * j + 1] for r in range(R)
             ]
 
             def rows(base):
@@ -747,6 +784,39 @@
                 old = att[j, b * BS : (b + 1) * BS, :].astype(jnp.float32)
                 att[j, b * BS : (b + 1) * BS, :] = jnp.where(here, row, old).astype(jnp.bfloat16)
 
+    rows = tokens // chunks
+
+    def swap(sent, got, ssem, rsem, c):
+        return remote(sent.at[c], got.at[c], ssem.at[c], rsem.at[c], {"mp": 1 - mine})
+
+    for c in range(chunks):
+        cut = slice(c * rows, (c + 1) * rows)
+        acc = dot(att[0, cut, :], out_w[0:LANES, :])
+        for j in range(1, pairs):
+            acc = acc + dot(att[j, cut, :], out_w[j * LANES : (j + 1) * LANES, :])
+        mine1[c] = acc.astype(mine1.dtype)
+        swap(mine1, theirs1, s1, r1, c).start()
+    x = xs[pl.ds(me * per, per)].reshape(chunks, rows, width)
+    for c in range(chunks):
+        swap(mine1, theirs1, s1, r1, c).wait_recv()
+        summed = mine1[c].astype(jnp.float32) + theirs1[c].astype(jnp.float32)
+        norm = layer_norm(x[c].astype(jnp.float32) + summed, gain1[...])
+        norm = norm.astype(jnp.bfloat16)
+        normed[c] = norm
+        v = dot(norm, up_w[...])
+        hidden = (v * (1.0 + lax.erf(v * (0.5**0.5))) * 0.5).astype(jnp.bfloat16)
+        mine2[c] = dot(hidden, down_w[...]).astype(mine2.dtype)
+        swap(mine2, theirs2, s2, r2, c).start()
+    for c in range(chunks):
+        cut = slice(c * rows, (c + 1) * rows)
+        swap(mine2, theirs2, s2, r2, c).wait_recv()
+        summed = mine2[c].astype(jnp.float32) + theirs2[c].astype(jnp.float32)
+        out[cut, :] = layer_norm(normed[c].astype(jnp.float32) + summed, gain2[...]).astype(
+            jnp.bfloat16
+        )
+    for c in range(chunks):
+        swap(mine1, theirs1, s1, r1, c).wait_send()
+        swap(mine2, theirs2, s2, r2, c).wait_send()
     for t in range(trees):
         onward(t, 0, 0, 0, lambda copy: copy.wait_send())
     for t, slot, dx, dy in order:
@@ -914,7 +984,18 @@
     )
 
 
-def attend_gathered(states, qkv_weight, global_ids, random_owner, random_local):
+def layer_gathered(
+    states,
+    qkv_weight,
+    out_weight,
+    up_weight,
+    down_weight,
+    attn_gain,
+    mlp_gain,
+    global_ids,
+    random_owner,
+    random_local,
+):
     tokens, width = states.shape
     inner = qkv_weight.shape[2]
     heads = inner // HD
@@ -925,13 +1006,26 @@
     trees = len(TREES)
     piece = tokens // (2 * trees)
     chunk = 8 * BS
+    chunks = CHUNKS
+    rows = tokens // chunks
     bf = jnp.bfloat16
     dma = pltpu.SemaphoreType.DMA
+    operands = (
+        states.reshape(2 * trees, piece, width),
+        qkv_weight,
+        random_owner.transpose(0, 3, 1, 2),
+        random_local.transpose(0, 3, 1, 2),
+        global_ids,
+        out_weight,
+        up_weight,
+        down_weight,
+        attn_gain.reshape(1, width),
+        mlp_gain.reshape(1, width),
+    )
     return pl.pallas_call(
-        functools.partial(gather_kernel, n, heads, blocks, g_count),
-        out_shape=jax.ShapeDtypeStruct((pairs, tokens, LANES), bf),
-        in_specs=[pl.BlockSpec(memory_space=pltpu.HBM)] * 2
-        + [pl.BlockSpec(memory_space=pltpu.SMEM)] * 3,
+        functools.partial(gather_kernel, n, heads, blocks, g_count, chunks),
+        out_shape=jax.ShapeDtypeStruct((tokens, width), bf),
+        in_specs=[pl.BlockSpec(memory_space=pltpu.HBM)] * len(operands),
         out_specs=pl.BlockSpec(memory_space=pltpu.VMEM),
         scratch_shapes=[
             pltpu.VMEM((n * 2 * trees, piece, width), bf),
@@ -942,25 +1036,25 @@
             pltpu.VMEM((n * tokens // chunk, 2 * BS, chunk), jnp.float32),
             pltpu.VMEM((BS, LANES), bf),
             pltpu.VMEM((pairs * g_count, BS, LANES), bf),
-            pltpu.VMEM((8, LANES), jnp.float32),
+            pltpu.SMEM((1, R, blocks, heads), jnp.int32),
+            pltpu.SMEM((1, R, blocks, heads), jnp.int32),
+            pltpu.SMEM(global_ids.shape, jnp.int32),
+            pltpu.VMEM((pairs, tokens, LANES), bf),
+            pltpu.VMEM(out_weight.shape, bf),
+            pltpu.VMEM(up_weight.shape, bf),
+            pltpu.VMEM(down_weight.shape, bf),
+            pltpu.VMEM((1, width), jnp.float32),
+            pltpu.VMEM((1, width), jnp.float32),
         ]
+        + [pltpu.VMEM((chunks, rows, width), bf)] * 5
         + [dma((n * trees,))] * 7
-        + [dma((n,)), dma((pairs * g_count,)), dma((4,))],
-        cost_estimate=pl.CostEstimate(
-            flops=30_000_000_000, bytes_accessed=20_000_000, transcendentals=0
+        + [dma((n,)), dma((pairs * g_count,))]
+        + [dma((chunks,))] * 4
+        + [dma((len(operands) + 2,))],
+        compiler_params=pltpu.CompilerParams(
+            collective_id=0, has_side_effects=True, vmem_limit_bytes=48 * 1024 * 1024
         ),
-        compiler_params=pltpu.CompilerParams(
-            collective_id=0, has_side_effects=True, vmem_limit_bytes=40 * 1024 * 1024
-        ),
-    )(
-        pltpu.with_memory_space_constraint(
-            states.reshape(2 * trees, piece, width), pltpu.HBM
-        ),
-        pltpu.with_memory_space_constraint(qkv_weight, pltpu.HBM),
-        random_owner,
-        random_local,
-        global_ids,
-    )
+    )(*[pltpu.with_memory_space_constraint(a, pltpu.HBM) for a in operands])
 
 
 def gathers(states, qkv_weight, global_ids):
@@ -992,10 +1086,22 @@
     random_local,
 ):
     tokens, width = states.shape
+    if gathers(states, qkv_weight, global_ids):
+        return layer_gathered(
+            states,
+            qkv_weight,
+            out_weight,
+            up_weight,
+            down_weight,
+            attn_gain,
+            mlp_gain,
+            global_ids,
+            random_owner,
+            random_local,
+        )
     bf = jnp.bfloat16
     dma = pltpu.SemaphoreType.DMA
-    attend = attend_gathered if gathers(states, qkv_weight, global_ids) else attend_requested
-    att = attend(states, qkv_weight, global_ids, random_owner, random_local)
+    att = attend_requested(states, qkv_weight, global_ids, random_owner, random_local)
 
     chunks = 4
     rows = tokens // chunks

time: 67.2 us -> 58.4 us (0.87)
  Pallas kernels: 62.4 us -> 54.8 us
  local copies, waits for them, and re-layouts: 4.39 us -> 3.3 us
    pallas_call x2 -> x1, Pallas kernels: 62.4 us -> 54.8 us  [layer_gathered(): pl.pallas_call(functools.partial(gather_kernel, n, heads, blocks, g_count...]
    unnamed x13 -> x1, local copies, waits for them, and re-layouts: 3.01 us -> 0.75 us
    reshape x2, local copies, waits for them, and re-layouts: 1.38 us -> 2.55 us  [the longest x1 1.28 us: layer_gathered(): mlp_gain.reshape(1, width)]
where the time goes in v2:
time: 58.4 us; the launch traced here: 58.1 us
  Pallas kernels  54.8 us (94%)
  local copies, waits for them, and re-layouts  3.3 us (6%)
    pallas_call x1, Pallas kernels, layer_gathered(): pl.pallas_call(functools.partial(gather_kernel, n, heads, blocks, g_count...  54.8 us
    reshape x1, local copies, waits for them, and re-layouts, layer_gathered(): mlp_gain.reshape(1, width)  1.28 us
    reshape x1, local copies, waits for them, and re-layouts, layer_gathered(): attn_gain.reshape(1, width)  1.27 us

profile of v2, /device:TPU:0, one launch (start us, length us, event | category | flops | bytes accessed | tf_op | source)
XLA Modules:
  0.0 58.1 jit_solution(12984244115480135048)
XLA Ops:
  0.0 1.3 %reshape.10.gain1_hbm = f32[1,768]{1,0:T(1,128)} reshape(f32[768]{0:T(1024)} %param.15) | data formatting | bytes 6144 | tf_op jit(solution)/shard_map/reshape | solution.py:1022
  1.3 1.3 %reshape.11.gain2_hbm = f32[1,768]{1,0:T(1,128)} reshape(f32[768]{0:T(1024)} %param.16) | data formatting | bytes 6144 | tf_op jit(solution)/shard_map/reshape | solution.py:1023
  2.5 54.8 %shard_map.100 = bf16[256,768]{1,0:T(8,128)(2,1)S(1)} custom-call(bf16[8,32,768]{2,1,0:T(8,128)(2,1)} %bitcast.3, bf16[3,768,384]{2,1,0:T(8,128)(2,1)} %weight_hbm.1, s32[1,3,4,6]{3,2,1,0:T(4,128)} %bitcast.4, s32[1,3,4,6]{3,2,1,0:T(4,128)} %bitcast.5, s32[2]{0:T(128)} %gids_hbm.1, bf16[384,768]{1,0:T(8,128)(2,1)} %out_hbm.1, bf16[768,1536]{1,0:T(8,128)(2,1)} %up_hbm.1, ...), custom_call_target="tpu_custom_call" | custom-call | tf_op jit(solution)/shard_map/pallas_call | solution.py:1025
  57.3 0.7 %copy.12 = bf16[256,768]{1,0:T(8,128)(2,1)} copy(bf16[256,768]{1,0:T(8,128)(2,1)S(1)} %shard_map.100) | data formatting | bytes 786432

commit v3 on v2

--- a/solution.py
+++ b/solution.py
@@ -442,7 +442,7 @@
     (-2.0, 5.0, 3.5, 13.5),
     (-1.5, 2.0, 7.5, 11.0),
 )
-LAG = 3
+LAG = 6
 CHUNKS = 2
 
 
@@ -493,6 +493,8 @@
     kv,
     q_all,
     wide,
+    scores,
+    weights,
     gmine,
     gout,
     owner,
@@ -534,7 +536,6 @@
     width = xs.shape[2]
     tokens = per * piece
     depth = n // 4
-    units = pairs * g_count
     x_at, y_at, z_at = lax.rem(me, 2), lax.rem(me // 2, 2), me // 4
 
     def remote(src, dst, ssem, rsem, where):
@@ -547,16 +548,6 @@
             device_id_type=MESH,
         )
 
-    def peer(k):
-        return lax.rem(me + k, n)
-
-    def each_peer(body):
-        def step(k, carry):
-            body(peer(k))
-            return carry
-
-        lax.fori_loop(1, n, step, 0)
-
     def plane(slot):
         if slot == 0:
             return z_at
@@ -574,11 +565,9 @@
         at = xs.at[(shard * 2 + mine) * trees + t]
         return remote(at, at, ssem.at[shard * trees + t], r_ici.at[shard * trees + t], {"seq": d})
 
-    def across(shard, t, core):
-        at = xs.at[(shard * 2 + core) * trees + t]
-        return remote(
-            at, at, s_mp.at[shard * trees + t], r_mp.at[shard * trees + t], {"mp": 1 - mine}
-        )
+    def across(shard, core):
+        at = xs.at[pl.ds((shard * 2 + core) * trees, trees)]
+        return remote(at, at, s_mp.at[shard], r_mp.at[shard], {"mp": 1 - mine})
 
     x_peer = me + 1 - 2 * x_at
     y_peer = me + 2 - 4 * y_at
@@ -601,8 +590,6 @@
                     go_down = go_down & (source > z_at)
                 pl.when(go_up)(lambda: act(ici(shard, t, s_up, up)))
                 pl.when(go_down)(lambda: act(ici(shard, t, s_down, down)))
-        if slot or dx or dy:
-            act(across(shard, t, mine))
 
     order = arrivals(depth)
 
@@ -659,8 +646,7 @@
 
     def finish(place):
         shard = shard_of(*place)
-        for t in range(trees):
-            across(shard, t, 1 - mine).wait_recv()
+        across(shard, 1 - mine).wait_recv()
         project(shard)
 
     for t, slot, dx, dy in order:
@@ -673,6 +659,7 @@
         place = (slot, dx, dy)
         left[place] = left.get(place, trees) - 1
         if left[place] == 0:
+            across(shard, mine).start()
             waiting.append((LAG, place))
     for _, place in waiting:
         finish(place)
@@ -689,16 +676,24 @@
     def together(out):
         return jnp.where(low, out[0:BS], out[BS : 2 * BS]).astype(jnp.bfloat16)
 
-    chunk = wide.shape[2]
+    spot = lax.rem(me, 4)
+    final = n - 1
+    steps, _, chunk = wide.shape
     per_chunk = chunk // BS
-    steps = wide.shape[0]
+
+    def fold(best, s, join):
+        for c in range(0, s.shape[1], LANES):
+            best = join(best, s[:, c : c + LANES])
+        return best
 
     def share():
-        j, g = me // g_count, lax.rem(me, g_count)
+        first_block = spot < pairs
+        j = jnp.where(first_block, spot, z_at)
+        block = jnp.where(first_block, gids[0], gids[1])
         k_cut = pl.ds(pl.multiple_of(j * LANES, LANES), LANES)
         v_cut = pl.ds(pl.multiple_of(inner + j * LANES, LANES), LANES)
         rows = BS // piece
-        x = xs[pl.ds(gids[g] * rows, rows)].reshape(BS, width)
+        x = xs[pl.ds(block * rows, rows)].reshape(BS, width)
         q = dot(x, wq[:, k_cut]).astype(jnp.bfloat16).astype(jnp.float32) * scaling
         q2 = split(q.astype(jnp.bfloat16))
 
@@ -706,9 +701,11 @@
             keys = kv[pl.ds(c * per_chunk, per_chunk), :, k_cut].reshape(chunk, LANES)
             s = dot_t(q2, keys)
             wide[c] = s
-            return jnp.maximum(best, jnp.max(s, axis=-1, keepdims=True))
-
-        high = lax.fori_loop(0, steps, score, jnp.full((2 * BS, 1), NEGATIVE, jnp.float32))
+            return fold(best, s, jnp.maximum)
+
+        best = jnp.full((2 * BS, LANES), NEGATIVE, jnp.float32)
+        best = lax.fori_loop(0, steps, score, best, unroll=True)
+        high = jnp.max(best, axis=-1, keepdims=True)
 
         def add(c, so_far):
             values = kv[pl.ds(c * per_chunk, per_chunk), :, v_cut].reshape(chunk, LANES)
@@ -717,72 +714,89 @@
             e_low = (e - e_high.astype(jnp.float32)).astype(jnp.bfloat16)
             return (
                 so_far[0] + dot(e_high, values) + dot(e_low, values),
-                so_far[1] + jnp.sum(e, axis=-1, keepdims=True),
+                fold(so_far[1], e, jnp.add),
             )
 
-        zero = (jnp.zeros((2 * BS, LANES), jnp.float32), jnp.zeros((2 * BS, 1), jnp.float32))
-        summed, total = lax.fori_loop(0, steps, add, zero)
-        done = together(summed / total)
-        gmine[...] = done
-        gout[me] = done
-        each_peer(lambda d: gout_copy(d, me).start())
-
-    def gout_copy(d, unit):
-        return remote(gmine, gout.at[unit], s_gout.at[d], r_gout.at[unit], {"seq": d})
-
-    def guarded(who, body):
-        if units < n:
-            pl.when(who < units)(body)
-        else:
-            body()
-
-    guarded(me, share)
+        zero = jnp.zeros((2 * BS, LANES), jnp.float32)
+        summed, total = lax.fori_loop(0, steps, add, (zero, zero), unroll=True)
+        gmine[...] = together(summed / jnp.sum(total, axis=-1, keepdims=True))
+
+        def to_plane():
+            for k in range(1, 4):
+                gout_copy(spot, k).start()
+
+        pl.when(first_block)(to_plane)
+        pl.when(spot >= pairs)(lambda: last_copy(z_at).start())
+
+    def gout_copy(unit, k):
+        d = z_at * 4 + lax.rem(spot + k, 4)
+        return remote(gmine, gout.at[unit], s_gout.at[k], r_gout.at[unit], {"seq": d})
+
+    def last_copy(unit):
+        at = pairs + unit
+        return remote(gmine, gout.at[at], s_gout.at[0], r_gout.at[at], {"seq": final})
+
+    shares = (spot < pairs) | ((spot == 3) & (z_at < pairs))
+    pl.when(shares)(share)
 
     slot_lane = lax.broadcasted_iota(jnp.int32, (1, 3 * BS), 1)
     last = n * blocks - 1
 
-    def block_step(b, carry):
+    def rows_of(b, j, base):
+        first = me * blocks + b
+        near = [jnp.maximum(first - 1, 0), first, jnp.minimum(first + 1, last)]
+        one = [owner[0, r, b, 2 * j] * blocks + local[0, r, b, 2 * j] for r in range(R)]
+        two = [owner[0, r, b, 2 * j + 1] * blocks + local[0, r, b, 2 * j + 1] for r in range(R)]
+        cut = slice(base + j * LANES, base + (j + 1) * LANES)
+        return jnp.concatenate(
+            [kv[at, :, cut] for at in near]
+            + [jnp.where(low, kv[a, :, cut], kv[c, :, cut]) for a, c in zip(one, two)]
+            + [kv[gids[g], :, cut] for g in range(g_count)],
+            axis=0,
+        )
+
+    for b in range(blocks):
         first = me * blocks + b
         start = jnp.where(first == 0, BS, 0)
         stop = jnp.where(first == last, 2 * BS, 3 * BS)
         bias = jnp.where((slot_lane < start) | (slot_lane >= stop), NEGATIVE, 0.0)
-        near = [jnp.maximum(first - 1, 0), first, jnp.minimum(first + 1, last)]
-        ends = [gids[g] for g in range(g_count)]
         for j in range(pairs):
-            one = [
-                owner[0, r, b, 2 * j] * blocks + local[0, r, b, 2 * j] for r in range(R)
-            ]
-            two = [
-                owner[0, r, b, 2 * j + 1] * blocks + local[0, r, b, 2 * j + 1] for r in range(R)
-            ]
-
-            def rows(base):
-                cut = slice(base + j * LANES, base + (j + 1) * LANES)
-                return jnp.concatenate(
-                    [kv[at, :, cut] for at in near]
-                    + [jnp.where(low, kv[a, :, cut], kv[c, :, cut]) for a, c in zip(one, two)]
-                    + [kv[at, :, cut] for at in ends],
-                    axis=0,
-                )
-
-            q = q_all[pl.ds(pl.multiple_of(b * BS, BS), BS), j * LANES : (j + 1) * LANES]
-            s = dot_t(split(q), rows(0))
-            s = jnp.concatenate([s[:, 0 : 3 * BS] + bias, s[:, 3 * BS :]], axis=1)
+            q = q_all[b * BS : (b + 1) * BS, j * LANES : (j + 1) * LANES]
+            s = dot_t(split(q), rows_of(b, j, 0))
+            scores[b * pairs + j, :, 0 : 3 * BS] = s[:, 0 : 3 * BS] + bias
+            scores[b * pairs + j, :, 3 * BS :] = s[:, 3 * BS :]
+
+    def weigh(i, carry):
+        for part in range(2):
+            cut = slice(part * BS, (part + 1) * BS)
+            s = scores[i, cut]
             e = jnp.exp(s - jnp.max(s, axis=-1, keepdims=True))
-            w = (e * (1.0 / jnp.sum(e, axis=-1, keepdims=True))).astype(jnp.bfloat16)
-            att[j, pl.ds(pl.multiple_of(b * BS, BS), BS), :] = together(dot(w, rows(inner)))
+            share_of = 1.0 / jnp.sum(e, axis=-1, keepdims=True)
+            weights[i, cut] = (e * share_of).astype(jnp.bfloat16)
         return carry
 
-    lax.fori_loop(0, blocks, block_step, 0)
-
-    each_peer(lambda d: guarded(d, lambda: gout_copy(d, d).wait_recv()))
+    lax.fori_loop(0, blocks * pairs, weigh, 0, unroll=6)
+
+    for b in range(blocks):
+        for j in range(pairs):
+            mixed = dot(weights[b * pairs + j], rows_of(b, j, inner))
+            att[j, b * BS : (b + 1) * BS, :] = together(mixed)
+
+    for unit in range(pairs):
+        pl.when(spot != unit)(lambda unit=unit: gout_copy(unit, 1).wait_recv())
     for j in range(pairs):
-        for g in range(g_count):
-            row = gout[j * g_count + g].astype(jnp.float32)
-            for b in range(blocks):
-                here = gids[g] == me * blocks + b
-                old = att[j, b * BS : (b + 1) * BS, :].astype(jnp.float32)
-                att[j, b * BS : (b + 1) * BS, :] = jnp.where(here, row, old).astype(jnp.bfloat16)
+        row = jnp.where(spot == j, gmine[...], gout[j])
+        for b in range(blocks):
+            cut = slice(b * BS, (b + 1) * BS)
+            here = gids[0] == me * blocks + b
+            att[j, cut, :] = jnp.where(here, row, att[j, cut, :])
+
+    def take_last():
+        for unit in range(pairs):
+            last_copy(unit).wait_recv()
+            att[unit, (blocks - 1) * BS : blocks * BS, :] = gout[pairs + unit]
+
+    pl.when(me == final)(take_last)
 
     rows = tokens // chunks
 
@@ -821,7 +835,15 @@
         onward(t, 0, 0, 0, lambda copy: copy.wait_send())
     for t, slot, dx, dy in order:
         onward(t, slot, dx, dy, lambda copy: copy.wait_send())
-    each_peer(lambda d: guarded(me, lambda: gout_copy(d, me).wait_send()))
+    for place in left:
+        across(shard_of(*place), mine).wait_send()
+
+    def drain():
+        for k in range(1, 4):
+            gout_copy(spot, k).wait_send()
+
+    pl.when(spot < pairs)(drain)
+    pl.when((spot == 3) & (z_at < pairs))(lambda: last_copy(z_at).wait_send())
 
 
 def tail_kernel(
@@ -1005,7 +1027,7 @@
     n = lax.axis_size("seq")
     trees = len(TREES)
     piece = tokens // (2 * trees)
-    chunk = 8 * BS
+    chunk = 16 * BS
     chunks = CHUNKS
     rows = tokens // chunks
     bf = jnp.bfloat16
@@ -1034,6 +1056,8 @@
             pltpu.VMEM((n * blocks, BS, 2 * inner), bf),
             pltpu.VMEM((tokens, inner), bf),
             pltpu.VMEM((n * tokens // chunk, 2 * BS, chunk), jnp.float32),
+            pltpu.VMEM((blocks * pairs, 2 * BS, (3 + R + g_count) * BS), jnp.float32),
+            pltpu.VMEM((blocks * pairs, 2 * BS, (3 + R + g_count) * BS), bf),
             pltpu.VMEM((BS, LANES), bf),
             pltpu.VMEM((pairs * g_count, BS, LANES), bf),
             pltpu.SMEM((1, R, blocks, heads), jnp.int32),
@@ -1047,8 +1071,9 @@
             pltpu.VMEM((1, width), jnp.float32),
         ]
         + [pltpu.VMEM((chunks, rows, width), bf)] * 5
-        + [dma((n * trees,))] * 7
-        + [dma((n,)), dma((pairs * g_count,))]
+        + [dma((n * trees,))] * 4
+        + [dma((n,)), dma((n * trees,)), dma((n,))]
+        + [dma((4,)), dma((pairs * g_count,))]
         + [dma((chunks,))] * 4
         + [dma((len(operands) + 2,))],
         compiler_params=pltpu.CompilerParams(
@@ -1062,12 +1087,15 @@
     n = lax.axis_size("seq")
     inner = qkv_weight.shape[2]
     held = n * tokens * (width + 2 * inner) * 2
-    units = inner // LANES * global_ids.shape[0]
+    pairs = inner // LANES
     return (
         n % 4 == 0
+        and global_ids.shape[0] == 2
+        and pairs < 4
+        and pairs < n // 4
         and lax.axis_size("mp") == 2
         and held <= 24 * 1024 * 1024
-        and units <= n
+        and n * tokens % (16 * BS) == 0
         and tokens % (2 * len(TREES) * 16) == 0
         and 2 * inner % 256 == 0
     )

time: 58.4 us -> 52.2 us (0.89)
  Pallas kernels: 54.8 us -> 48.6 us
    pallas_call x1, Pallas kernels: 54.8 us -> 48.6 us  [layer_gathered(): pl.pallas_call(functools.partial(gather_kernel, n, heads, blocks, g_count...]
where the time goes in v3:
time: 52.2 us; the launch traced here: 51.9 us
  Pallas kernels  48.6 us (93%)
  local copies, waits for them, and re-layouts  3.3 us (6%)
    pallas_call x1, Pallas kernels, layer_gathered(): pl.pallas_call(functools.partial(gather_kernel, n, heads, blocks, g_count...  48.6 us
    reshape x1, local copies, waits for them, and re-layouts, layer_gathered(): mlp_gain.reshape(1, width)  1.28 us
    reshape x1, local copies, waits for them, and re-layouts, layer_gathered(): attn_gain.reshape(1, width)  1.27 us

profile of v3, /device:TPU:0, one launch (start us, length us, event | category | flops | bytes accessed | tf_op | source)
XLA Modules:
  0.0 51.9 jit_solution(11909789963184783253)
XLA Ops:
  0.0 1.3 %reshape.10.gain1_hbm = f32[1,768]{1,0:T(1,128)} reshape(f32[768]{0:T(1024)} %param.15) | data formatting | bytes 6144 | tf_op jit(solution)/shard_map/reshape | solution.py:1044
  1.3 1.3 %reshape.11.gain2_hbm = f32[1,768]{1,0:T(1,128)} reshape(f32[768]{0:T(1024)} %param.16) | data formatting | bytes 6144 | tf_op jit(solution)/shard_map/reshape | solution.py:1045
  2.5 48.6 %shard_map.100 = bf16[256,768]{1,0:T(8,128)(2,1)S(1)} custom-call(bf16[8,32,768]{2,1,0:T(8,128)(2,1)} %bitcast.3, bf16[3,768,384]{2,1,0:T(8,128)(2,1)} %weight_hbm.1, s32[1,3,4,6]{3,2,1,0:T(4,128)} %bitcast.4, s32[1,3,4,6]{3,2,1,0:T(4,128)} %bitcast.5, s32[2]{0:T(128)} %gids_hbm.1, bf16[384,768]{1,0:T(8,128)(2,1)} %out_hbm.1, bf16[768,1536]{1,0:T(8,128)(2,1)} %up_hbm.1, ...), custom_call_target="tpu_custom_call" | custom-call | tf_op jit(solution)/shard_map/pallas_call | solution.py:1047
  51.2 0.7 %copy.12 = bf16[256,768]{1,0:T(8,128)(2,1)} copy(bf16[256,768]{1,0:T(8,128)(2,1)S(1)} %shard_map.100) | data formatting | bytes 786432

commit v4 on v3

--- a/solution.py
+++ b/solution.py
@@ -437,24 +437,27 @@
 TREES = ("zxy", "zyx", "yzx", "xzy")
 PLACES = ((0, 0), (1, 0), (0, 1), (1, 1))
 TURNS = (
-    (-8.5, -3.0, -1.5, 10.5),
-    (-5.5, 3.0, 0.0, 8.0),
-    (-2.0, 5.0, 3.5, 13.5),
-    (-1.5, 2.0, 7.5, 11.0),
+    (-21.5, -8.5, -4.5, 11.5),
+    (-15.0, 1.0, -2.5, 14.5),
+    (-17.5, 0.0, -6.5, 11.5),
+    (-13.0, -3.0, 2.5, 15.0),
 )
-LAG = 6
+PAUSES = (7.5, 9.5, 13.5, 18.0)
+ROUND = 9.0
 CHUNKS = 2
 
 
 def arrivals(depth):
-    pieces = [
-        (3.5 * slot + TURNS[t][p], t, slot, *PLACES[p])
-        for t in range(len(TREES))
-        for slot in range(depth)
-        for p in range(len(PLACES))
-        if slot or p
-    ]
-    return [piece[1:] for piece in sorted(pieces)]
+    steps = []
+    for slot in range(depth):
+        for p, (dx, dy) in enumerate(PLACES):
+            if not slot and not p:
+                continue
+            place = (slot, dx, dy)
+            turns = [ROUND * slot + row[p] for row in TURNS]
+            steps += [(turn, 0, t, place) for t, turn in enumerate(turns)]
+            steps.append((max(turns) + PAUSES[p], 1, 0, place))
+    return [step[1:] for step in sorted(steps)]
 
 
 def hops(tree, slot, dx, dy):
@@ -641,28 +644,18 @@
     ).astype(jnp.bfloat16)
     project(me)
 
-    waiting = []
     left = dict()
-
-    def finish(place):
+    for kind, t, place in order:
         shard = shard_of(*place)
-        across(shard, 1 - mine).wait_recv()
-        project(shard)
-
-    for t, slot, dx, dy in order:
-        shard = shard_of(slot, dx, dy)
+        if kind:
+            across(shard, 1 - mine).wait_recv()
+            project(shard)
+            continue
         ici(shard, t, s_x, x_peer).wait_recv()
-        onward(t, slot, dx, dy, lambda copy: copy.start())
-        waiting = [(count - 1, place) for count, place in waiting]
-        while waiting and waiting[0][0] <= 0:
-            finish(waiting.pop(0)[1])
-        place = (slot, dx, dy)
+        onward(t, *place, lambda copy: copy.start())
         left[place] = left.get(place, trees) - 1
         if left[place] == 0:
             across(shard, mine).start()
-            waiting.append((LAG, place))
-    for _, place in waiting:
-        finish(place)
     for load in loads[4:]:
         load.wait()
 
@@ -814,7 +807,7 @@
     for c in range(chunks):
         swap(mine1, theirs1, s1, r1, c).wait_recv()
         summed = mine1[c].astype(jnp.float32) + theirs1[c].astype(jnp.float32)
-        norm = layer_norm(x[c].astype(jnp.float32) + summed, gain1[...])
+        norm = layer_norm(x[c].astype(jnp.float32) + summed, gain1[...].reshape(1, width))
         norm = norm.astype(jnp.bfloat16)
         normed[c] = norm
         v = dot(norm, up_w[...])
@@ -825,7 +818,7 @@
         cut = slice(c * rows, (c + 1) * rows)
         swap(mine2, theirs2, s2, r2, c).wait_recv()
         summed = mine2[c].astype(jnp.float32) + theirs2[c].astype(jnp.float32)
-        out[cut, :] = layer_norm(normed[c].astype(jnp.float32) + summed, gain2[...]).astype(
+        out[cut, :] = layer_norm(normed[c].astype(jnp.float32) + summed, gain2[...].reshape(1, width)).astype(
             jnp.bfloat16
         )
     for c in range(chunks):
@@ -833,8 +826,9 @@
         swap(mine2, theirs2, s2, r2, c).wait_send()
     for t in range(trees):
         onward(t, 0, 0, 0, lambda copy: copy.wait_send())
-    for t, slot, dx, dy in order:
-        onward(t, slot, dx, dy, lambda copy: copy.wait_send())
+    for kind, t, place in order:
+        if not kind:
+            onward(t, *place, lambda copy: copy.wait_send())
     for place in left:
         across(shard_of(*place), mine).wait_send()
 
@@ -1041,8 +1035,8 @@
         out_weight,
         up_weight,
         down_weight,
-        attn_gain.reshape(1, width),
-        mlp_gain.reshape(1, width),
+        attn_gain,
+        mlp_gain,
     )
     return pl.pallas_call(
         functools.partial(gather_kernel, n, heads, blocks, g_count, chunks),
@@ -1067,8 +1061,8 @@
             pltpu.VMEM(out_weight.shape, bf),
             pltpu.VMEM(up_weight.shape, bf),
             pltpu.VMEM(down_weight.shape, bf),
-            pltpu.VMEM((1, width), jnp.float32),
-            pltpu.VMEM((1, width), jnp.float32),
+            pltpu.VMEM((width,), jnp.float32),
+            pltpu.VMEM((width,), jnp.float32),
         ]
         + [pltpu.VMEM((chunks, rows, width), bf)] * 5
         + [dma((n * trees,))] * 4

time: 52.2 us -> 46.4 us (0.89)
  Pallas kernels: 48.6 us -> 45.5 us
  local copies, waits for them, and re-layouts: 3.3 us -> 0.75 us
    pallas_call x1, Pallas kernels: 48.6 us -> 45.5 us  [layer_gathered(): pl.pallas_call(functools.partial(gather_kernel, n, heads, blocks, g_count...]
    reshape x2 -> x0, local copies, waits for them, and re-layouts: 2.55 us -> none  [the longest x1 1.28 us: layer_gathered(): mlp_gain.reshape(1, width)]
where the time goes in v4:
time: 46.4 us; the launch traced here: 46.3 us
  Pallas kernels  45.5 us (98%)
  local copies, waits for them, and re-layouts  0.75 us (2%)
    pallas_call x1, Pallas kernels, layer_gathered(): pl.pallas_call(functools.partial(gather_kernel, n, heads, blocks, g_count...  45.5 us

profile of v4, /device:TPU:0, one launch (start us, length us, event | category | flops | bytes accessed | tf_op | source)
XLA Modules:
  0.0 46.3 jit_solution(5899329137775646915)
XLA Ops:
  0.0 45.5 %shard_map.100 = bf16[256,768]{1,0:T(8,128)(2,1)S(1)} custom-call(bf16[8,32,768]{2,1,0:T(8,128)(2,1)} %bitcast.3, bf16[3,768,384]{2,1,0:T(8,128)(2,1)} %weight_hbm.1, s32[1,3,4,6]{3,2,1,0:T(4,128)} %bitcast.4, s32[1,3,4,6]{3,2,1,0:T(4,128)} %bitcast.5, s32[2]{0:T(128)} %gids_hbm.1, bf16[384,768]{1,0:T(8,128)(2,1)} %out_hbm.1, bf16[768,1536]{1,0:T(8,128)(2,1)} %up_hbm.1, ...), custom_call_target="tpu_custom_call" | custom-call | tf_op jit(solution)/shard_map/pallas_call | solution.py:1041
  45.5 0.7 %copy.12 = bf16[256,768]{1,0:T(8,128)(2,1)} copy(bf16[256,768]{1,0:T(8,128)(2,1)S(1)} %shard_map.100) | data formatting | bytes 786432

commit v5 on v4

--- a/solution.py
+++ b/solution.py
@@ -445,6 +445,7 @@
 PAUSES = (7.5, 9.5, 13.5, 18.0)
 ROUND = 9.0
 CHUNKS = 2
+OWN = 16
 
 
 def arrivals(depth):
@@ -566,11 +567,11 @@
 
     def ici(shard, t, ssem, d):
         at = xs.at[(shard * 2 + mine) * trees + t]
-        return remote(at, at, ssem.at[shard * trees + t], r_ici.at[shard * trees + t], {"seq": d})
+        return remote(at, at, ssem.at[0], r_ici.at[shard * trees + t], {"seq": d})
 
     def across(shard, core):
         at = xs.at[pl.ds((shard * 2 + core) * trees, trees)]
-        return remote(at, at, s_mp.at[shard], r_mp.at[shard], {"mp": 1 - mine})
+        return remote(at, at, s_mp.at[0], r_mp.at[shard], {"mp": 1 - mine})
 
     x_peer = me + 1 - 2 * x_at
     y_peer = me + 2 - 4 * y_at
@@ -622,34 +623,46 @@
                 barrier, inc=1, device_id={"seq": d}, device_id_type=MESH
             )
         )
-    for load in loads[1:]:
+    for load in loads[1:4]:
         load.start()
     column = jnp.where(z_at < depth - 1, 1, 0) + jnp.where(z_at > 0, 1, 0)
     loads[0].wait()
     pl.semaphore_wait(barrier, 3 + column)
     for t in range(trees):
         onward(t, 0, 0, 0, lambda copy: copy.start())
-    for load in loads[1:4]:
-        load.wait()
-
-    def project(shard):
-        x = xs[pl.ds(shard * per, per)].reshape(tokens, width)
-        y = dot(x, wkv[...]).astype(jnp.bfloat16)
-        kv[pl.ds(shard * blocks, blocks)] = y.reshape(blocks, BS, 2 * inner)
-
-    x = xs[pl.ds(me * per, per)].reshape(tokens, width)
+    for load in loads[4:]:
+        load.start()
+
+    def project(*shards):
+        x = [xs[pl.ds(shard * per, per)].reshape(tokens, width) for shard in shards]
+        y = dot(jnp.concatenate(x, axis=0), wkv[...]).astype(jnp.bfloat16)
+        for i, shard in enumerate(shards):
+            part = y[i * tokens : (i + 1) * tokens]
+            kv[pl.ds(shard * blocks, blocks)] = part.reshape(blocks, BS, 2 * inner)
+
     scaling = HD ** (-0.5)
-    q_all[...] = (
-        dot(x, wq[...]).astype(jnp.bfloat16).astype(jnp.float32) * scaling
-    ).astype(jnp.bfloat16)
-    project(me)
+
+    def project_own():
+        for load in loads[1:4]:
+            load.wait()
+        x = xs[pl.ds(me * per, per)].reshape(tokens, width)
+        q = dot(x, wq[...]).astype(jnp.bfloat16).astype(jnp.float32) * scaling
+        q_all[...] = q.astype(jnp.bfloat16)
+        project(me)
 
     left = dict()
-    for kind, t, place in order:
+    ready = []
+    for i, (kind, t, place) in enumerate(order):
+        if i == OWN:
+            project_own()
         shard = shard_of(*place)
         if kind:
             across(shard, 1 - mine).wait_recv()
-            project(shard)
+            ready.append(shard)
+            after = [step[0] for step in order[i + 1 : i + 3]]
+            if after != [1, 1] or len(ready) == 2:
+                project(*ready)
+                ready = []
             continue
         ici(shard, t, s_x, x_peer).wait_recv()
         onward(t, *place, lambda copy: copy.start())
@@ -824,13 +837,23 @@
     for c in range(chunks):
         swap(mine1, theirs1, s1, r1, c).wait_send()
         swap(mine2, theirs2, s2, r2, c).wait_send()
-    for t in range(trees):
-        onward(t, 0, 0, 0, lambda copy: copy.wait_send())
-    for kind, t, place in order:
-        if not kind:
-            onward(t, *place, lambda copy: copy.wait_send())
-    for place in left:
-        across(shard_of(*place), mine).wait_send()
+    def drain_all(ssem, count):
+        at = xs.at[pl.ds(0, count)]
+        remote(at, at, ssem.at[0], r_mp.at[0], {"mp": 1 - mine}).wait_send()
+
+    taken = [(t, (0, 0, 0)) for t in range(trees)]
+    taken += [(t, place) for kind, t, place in order if not kind]
+    routes = [(hops(TREES[t], *place), place[0]) for t, place in taken]
+    for axis, ssem in (("x", s_x), ("y", s_y)):
+        drain_all(ssem, sum(axis in axes for (_, axes), _ in routes))
+    drain_all(s_mp, trees * len(left))
+    for z in range(depth):
+        here = [(via, slots(z, depth)[slot]) for (via, axes), slot in routes if "z" in axes]
+        rising = sum(via != "z" or source < z for via, source in here) if z < depth - 1 else 0
+        falling = sum(via != "z" or source > z for via, source in here) if z > 0 else 0
+        for count, ssem in ((rising, s_up), (falling, s_down)):
+            if count:
+                pl.when(z_at == z)(lambda ssem=ssem, count=count: drain_all(ssem, count))
 
     def drain():
         for k in range(1, 4):
@@ -1065,8 +1088,8 @@
             pltpu.VMEM((width,), jnp.float32),
         ]
         + [pltpu.VMEM((chunks, rows, width), bf)] * 5
-        + [dma((n * trees,))] * 4
-        + [dma((n,)), dma((n * trees,)), dma((n,))]
+        + [dma((1,))] * 5
+        + [dma((n * trees,)), dma((n,))]
         + [dma((4,)), dma((pairs * g_count,))]
         + [dma((chunks,))] * 4
         + [dma((len(operands) + 2,))],

time: 46.4 us -> 43.5 us (0.938)
  Pallas kernels: 45.5 us -> 42.6 us
    pallas_call x1, Pallas kernels: 45.5 us -> 42.6 us  [layer_gathered(): pl.pallas_call(functools.partial(gather_kernel, n, heads, blocks, g_count...]
where the time goes in v5:
time: 43.5 us; the launch traced here: 43.4 us
  Pallas kernels  42.6 us (98%)
  local copies, waits for them, and re-layouts  0.75 us (2%)
    pallas_call x1, Pallas kernels, layer_gathered(): pl.pallas_call(functools.partial(gather_kernel, n, heads, blocks, g_count...  42.6 us

profile of v5, /device:TPU:0, one launch (start us, length us, event | category | flops | bytes accessed | tf_op | source)
XLA Modules:
  0.0 43.4 jit_solution(8677492060440500247)
XLA Ops:
  0.0 42.6 %shard_map.100 = bf16[256,768]{1,0:T(8,128)(2,1)S(1)} custom-call(bf16[8,32,768]{2,1,0:T(8,128)(2,1)} %bitcast.3, bf16[3,768,384]{2,1,0:T(8,128)(2,1)} %weight_hbm.1, s32[1,3,4,6]{3,2,1,0:T(4,128)} %bitcast.4, s32[1,3,4,6]{3,2,1,0:T(4,128)} %bitcast.5, s32[2]{0:T(128)} %gids_hbm.1, bf16[384,768]{1,0:T(8,128)(2,1)} %out_hbm.1, bf16[768,1536]{1,0:T(8,128)(2,1)} %up_hbm.1, ...), custom_call_target="tpu_custom_call" | custom-call | tf_op jit(solution)/shard_map/pallas_call | solution.py:1064
  42.6 0.7 %copy.12 = bf16[256,768]{1,0:T(8,128)(2,1)} copy(bf16[256,768]{1,0:T(8,128)(2,1)S(1)} %shard_map.100) | data formatting | bytes 786432

commit v6 on v5

--- a/solution.py
+++ b/solution.py
@@ -781,7 +781,7 @@
             weights[i, cut] = (e * share_of).astype(jnp.bfloat16)
         return carry
 
-    lax.fori_loop(0, blocks * pairs, weigh, 0, unroll=6)
+    lax.fori_loop(0, blocks * pairs, weigh, 0, unroll=True)
 
     for b in range(blocks):
         for j in range(pairs):
@@ -807,7 +807,7 @@
     rows = tokens // chunks
 
     def swap(sent, got, ssem, rsem, c):
-        return remote(sent.at[c], got.at[c], ssem.at[c], rsem.at[c], {"mp": 1 - mine})
+        return remote(sent.at[c], got.at[c], ssem.at[0], rsem.at[c], {"mp": 1 - mine})
 
     for c in range(chunks):
         cut = slice(c * rows, (c + 1) * rows)
@@ -834,9 +834,8 @@
         out[cut, :] = layer_norm(normed[c].astype(jnp.float32) + summed, gain2[...].reshape(1, width)).astype(
             jnp.bfloat16
         )
-    for c in range(chunks):
-        swap(mine1, theirs1, s1, r1, c).wait_send()
-        swap(mine2, theirs2, s2, r2, c).wait_send()
+    remote(mine1, theirs1, s1.at[0], r1.at[0], {"mp": 1 - mine}).wait_send()
+    remote(mine2, theirs2, s2.at[0], r2.at[0], {"mp": 1 - mine}).wait_send()
     def drain_all(ssem, count):
         at = xs.at[pl.ds(0, count)]
         remote(at, at, ssem.at[0], r_mp.at[0], {"mp": 1 - mine}).wait_send()
@@ -1091,7 +1090,7 @@
         + [dma((1,))] * 5
         + [dma((n * trees,)), dma((n,))]
         + [dma((4,)), dma((pairs * g_count,))]
-        + [dma((chunks,))] * 4
+        + [dma((1,)), dma((chunks,))] * 2
         + [dma((len(operands) + 2,))],
         compiler_params=pltpu.CompilerParams(
             collective_id=0, has_side_effects=True, vmem_limit_bytes=48 * 1024 * 1024

time: 43.5 us -> 43.5 us (level)
  no operation moved by 1% of the time
where the time goes in v6:
time: 43.5 us; the launch traced here: 43.4 us
  Pallas kernels  42.6 us (98%)
  local copies, waits for them, and re-layouts  0.75 us (2%)
    pallas_call x1, Pallas kernels, layer_gathered(): pl.pallas_call(functools.partial(gather_kernel, n, heads, blocks, g_count...  42.6 us

profile of v6, /device:TPU:0, one launch (start us, length us, event | category | flops | bytes accessed | tf_op | source)
XLA Modules:
  0.0 43.4 jit_solution(3475070545916112599)
XLA Ops:
  0.0 42.6 %shard_map.100 = bf16[256,768]{1,0:T(8,128)(2,1)S(1)} custom-call(bf16[8,32,768]{2,1,0:T(8,128)(2,1)} %bitcast.3, bf16[3,768,384]{2,1,0:T(8,128)(2,1)} %weight_hbm.1, s32[1,3,4,6]{3,2,1,0:T(4,128)} %bitcast.4, s32[1,3,4,6]{3,2,1,0:T(4,128)} %bitcast.5, s32[2]{0:T(128)} %gids_hbm.1, bf16[384,768]{1,0:T(8,128)(2,1)} %out_hbm.1, bf16[768,1536]{1,0:T(8,128)(2,1)} %up_hbm.1, ...), custom_call_target="tpu_custom_call" | custom-call | tf_op jit(solution)/shard_map/pallas_call | solution.py:1063
  42.6 0.7 %copy.12 = bf16[256,768]{1,0:T(8,128)(2,1)} copy(bf16[256,768]{1,0:T(8,128)(2,1)S(1)} %shard_map.100) | data formatting | bytes 786432
